TPU v7x, 32 devices: a 4x4x1 block of a 4x4x8 slice. The times are simulated.
32 devices in a mesh: dp: 1 (over z), tp: 4 (over y), fsdp: 8 (over x, core).
Axes of the slice: x: 4, y: 4, z: 1, core: 2. Of those that a mesh axis runs over, the one named last changes fastest.
The devices are a block of a 4x4x8 slice.
Arguments:
- hidden: bfloat16 [8, 1024, 2048], P(('dp', 'fsdp'))
- positions: int32 [1024], replicated
- norm_gain: float32 [2048], P('fsdp')
- w_query: bfloat16 [2048, 2048], P('fsdp', 'tp')
- w_key: bfloat16 [2048, 256], P('fsdp')
- w_value: bfloat16 [2048, 256], P('fsdp')
- w_gate: bfloat16 [2048, 16384], P('fsdp', 'tp')
- w_up: bfloat16 [2048, 16384], P('fsdp', 'tp')
- w_out: bfloat16 [2048, 2048], P('tp', 'fsdp')
- w_down: bfloat16 [16384, 2048], P('tp', 'fsdp')
Outputs:
- output: bfloat16 [8, 1024, 2048], P(('dp', 'fsdp'))
All inputs are finite; a program needn't handle non-finite values.
Results may differ from a plain program's by a relative error of at most 0.00869661.
Values are sent between devices in bfloat16 or wider.
A program may use at most 768 MiB of HBM per device.

v0:
```python
import jax
import jax.numpy as jnp
from jax import lax
from jax.sharding import PartitionSpec as P

Q_BLOCK = 512
NORM_EPS = 1e-6


def rope_tables(positions, head_dim):
    inv_freq = 10000.0 ** (-jnp.arange(0, head_dim, 2, dtype=jnp.float32) / head_dim)
    angles = positions.astype(jnp.float32)[:, None] * inv_freq[None, :]
    angles = jnp.concatenate([angles, angles], axis=-1)
    return jnp.cos(angles), jnp.sin(angles)


def rope_rotate(vectors, cos_t, sin_t):
    half_dim = vectors.shape[-1] // 2
    rotated = jnp.concatenate([-vectors[..., half_dim:], vectors[..., :half_dim]], axis=-1)
    return vectors * cos_t + rotated * sin_t


def layer_norm(hidden, gain_vec):
    row_f32 = hidden.astype(jnp.float32)
    centered = row_f32 - jnp.mean(row_f32, axis=-1, keepdims=True)
    variance = jnp.mean(centered * centered, axis=-1, keepdims=True)
    return (centered * lax.rsqrt(variance + NORM_EPS) * gain_vec).astype(jnp.bfloat16)


def project(operand, weight):
    return jnp.einsum("bsn,nm->bsm", operand, weight, preferred_element_type=jnp.float32)


def causal_attention(query_rot, key_rot, values):
    batch = query_rot.shape[0]
    seq_len = query_rot.shape[1]
    n_heads = query_rot.shape[2]
    head_dim = query_rot.shape[3]
    q_block = min(Q_BLOCK, seq_len)
    score_scale = head_dim ** -0.5
    pieces = []
    for blk_idx in range(seq_len // q_block):
        blk_lo = blk_idx * q_block
        blk_hi = blk_lo + q_block
        scores = jnp.einsum("bshe,bte->bsht", query_rot[:, blk_lo:blk_hi], key_rot[:, :blk_hi], preferred_element_type=jnp.float32) * score_scale
        causal_mask = jnp.arange(blk_hi)[None, :] <= (blk_lo + jnp.arange(q_block))[:, None]
        scores = jnp.where(causal_mask[None, :, None, :], scores, -1e30)
        prob_rows = jax.nn.softmax(scores, axis=-1).astype(jnp.bfloat16)
        pieces.append(jnp.einsum("bsht,bte->bshe", prob_rows, values[:, :blk_hi], preferred_element_type=jnp.float32).astype(jnp.bfloat16))
    attn_out = jnp.concatenate(pieces, axis=1)
    return attn_out.reshape(batch, seq_len, n_heads * head_dim)


def solution(mesh):
    row_spec = P(("dp", "fsdp"), None, None)

    def local_layer(hidden, positions, norm_gain, w_query, w_key, w_value, w_gate, w_up, w_out, w_down):
        gain_full = lax.all_gather(norm_gain, "fsdp", axis=0, tiled=True)
        wq_full = lax.all_gather(w_query, "fsdp", axis=0, tiled=True)
        wk_full = lax.all_gather(w_key, "fsdp", axis=0, tiled=True)
        wv_full = lax.all_gather(w_value, "fsdp", axis=0, tiled=True)
        wg_full = lax.all_gather(w_gate, "fsdp", axis=0, tiled=True)
        wu_full = lax.all_gather(w_up, "fsdp", axis=0, tiled=True)
        wo_full = lax.all_gather(w_out, "fsdp", axis=1, tiled=True)
        wd_full = lax.all_gather(w_down, "fsdp", axis=1, tiled=True)
        batch = hidden.shape[0]
        seq_len = hidden.shape[1]
        head_dim = wk_full.shape[1]
        normed = layer_norm(hidden, gain_full)
        query_raw = project(normed, wq_full).astype(jnp.bfloat16)
        key_raw = project(normed, wk_full).astype(jnp.bfloat16)
        values = project(normed, wv_full).astype(jnp.bfloat16)
        gate_raw = project(normed, wg_full).astype(jnp.bfloat16)
        up_raw = project(normed, wu_full).astype(jnp.bfloat16)
        cos_t, sin_t = rope_tables(positions, head_dim)
        query_rot = rope_rotate(query_raw.reshape(batch, seq_len, -1, head_dim).astype(jnp.float32), cos_t[:, None, :], sin_t[:, None, :]).astype(jnp.bfloat16)
        key_rot = rope_rotate(key_raw.astype(jnp.float32), cos_t, sin_t).astype(jnp.bfloat16)
        attn_out = causal_attention(query_rot, key_rot, values)
        gated_act = (jax.nn.silu(gate_raw.astype(jnp.float32)) * up_raw.astype(jnp.float32)).astype(jnp.bfloat16)
        branch = project(attn_out, wo_full) + project(gated_act, wd_full)
        branch = lax.psum(branch.astype(jnp.bfloat16), "tp")
        return (hidden.astype(jnp.float32) + branch.astype(jnp.float32)).astype(jnp.bfloat16)

    in_specs = (row_spec, P(None), P("fsdp"), P("fsdp", "tp"), P("fsdp", None), P("fsdp", None), P("fsdp", "tp"), P("fsdp", "tp"), P("tp", "fsdp"), P("tp", "fsdp"))
    return jax.shard_map(local_layer, mesh=mesh, in_specs=in_specs, out_specs=row_spec, check_vma=False)
```

profile of v0, /device:TPU:97, one launch (start us, length us, event | category | flops | bytes accessed | tf_op | source)
XLA Modules:
  0.0 497.0 jit_solution(17761017341154522381)
XLA Ops:
  6.6 0.7 all-gather.11.cloned.1.call-update
  7.4 0.7 all-gather.13.cloned.1.call-update
  10.9 0.7 all-gather.21.cloned.1.call-update
  11.8 19.5 %all-gather = f32[8,1,256]{2,1,0:T(1,128)S(1)} all-gather(f32[1,1,256]{2,1,0:T(1,128)S(1)} %bitcast.74), channel_id=1, replica_groups=mesh['dp'=1,'tp'=4,'fsdp'=8] {'fsdp'}, dimensions={0}, use_global_device_ids=true | all-gather | bytes 9216 | tf_op jit(solution)/shard_map/all_gather | solution.py:58
  31.4 2.8 convert_reduce_fusion
  34.2 1.2 fusion.9
  35.5 1.2 iota_compare_fusion
  36.7 3.0 fusion.16
  39.7 3.8 convolution_convert_fusion.3
  43.7 5.1 %fusion.29 = (bf16[1024,256]{0,1:T(8,128)(2,1)}, f32[1024,256]{0,1:T(8,128)S(1)}, f32[1024,256]{0,1:T(8,128)S(1)}) fusion(bf16[1024,256]{0,1:T(8,128)(2,1)S(1)} %convolution_convert_fusion.3, f32[1024,128]{0,1:T(8,128)S(1)} %get-tuple-element.8, f32[1024,128]{0,1:T(8,128)S(1)} %get-tuple-element.7, f32[1024,128]{0,1:T(8,128)S(1)} %broadcast_multiply_fusion), kind=kLoop, calls=%fused_computation.46 | loop fusion | flops 1835008 | bytes 4718592 | tf_op jit(solution)/shard_map/convert_element_type | solution.py:77
  49.1 1.4 copy.25
  50.5 5.4 %all-gather.13.cloned.1.call-done = bf16[2048,256]{1,0:T(8,128)(2,1)} async-done(((bf16[256,256]{1,0:T(8,128)(2,1)}), bf16[2048,256]{1,0:T(8,128)(2,1)}) %all-gather.13.cloned.1.call-update) | async-done | bytes 1048592 | tf_op jit(solution)/shard_map/all_gather | solution.py:61
  55.9 4.5 convolution_convert_fusion.2
  60.5 19.5 %all-gather.9.cloned.1.call-done = bf16[2048,512]{1,0:T(8,128)(2,1)} async-done(((bf16[256,512]{1,0:T(8,128)(2,1)}), bf16[2048,512]{1,0:T(8,128)(2,1)}) %all-gather.9.cloned.1.call-update) | async-done | bytes 2097168 | tf_op jit(solution)/shard_map/all_gather | solution.py:59
  80.0 6.2 %convolution_convert_fusion = bf16[1024,512]{0,1:T(8,128)(2,1)} fusion(bf16[1024,2048]{1,0:T(8,128)(2,1)} %fusion.16, bf16[2048,512]{1,0:T(8,128)(2,1)} %all-gather.9.cloned.1.call-done), kind=kOutput, calls=%fused_computation.38 | convolution fusion | flops 2148007936 | bytes 7340032 | tf_op jit(solution)/shard_map/bsn,nm->bsm/dot_general | solution.py:31
  86.2 1.7 copy.22
  88.0 1.1 copy-done.1
  89.0 1.3 fusion.21
  90.4 3.5 fusion.50
  94.6 0.9 copy-done.8
  96.0 2.0 fusion.49
  98.0 1.0 fusion.27
  98.9 6.9 %all-gather.15.cloned.1.call-done = bf16[512,2048]{1,0:T(8,128)(2,1)} async-done(((bf16[512,256]{1,0:T(8,128)(2,1)}), bf16[512,2048]{1,0:T(8,128)(2,1)}) %all-gather.15.cloned.1.call-update) | async-done | bytes 2097168 | tf_op jit(solution)/shard_map/all_gather | solution.py:64
  105.9 7.2 %fusion.32 = f32[1024,2048]{1,0:T(8,128)} fusion(bf16[512,2048]{1,0:T(8,128)(2,1)} %all-gather.15.cloned.1.call-done, bf16[1,512,512]{1,2,0:T(8,128)(2,1)S(1)} %bitcast.77, bf16[1,512,512]{1,2,0:T(8,128)(2,1)S(1)} %bitcast.76), kind=kOutput, calls=%fused_computation.53 | convolution fusion | flops 2149580800 | bytes 11534336 | tf_op jit(solution)/shard_map/bsn,nm->bsm/dot_general | solution.py:31
  113.1 77.8 %all-gather.17.cloned.1.call-done = bf16[2048,4096]{1,0:T(8,128)(2,1)} async-done(((bf16[256,4096]{1,0:T(8,128)(2,1)}), bf16[2048,4096]{1,0:T(8,128)(2,1)}) %all-gather.17.cloned.1.call-update) | async-done | bytes 16777232 | tf_op jit(solution)/shard_map/all_gather | solution.py:62
  190.9 22.9 %fusion.51 = bf16[1024,4096]{1,0:T(8,128)(2,1)} fusion(bf16[1024,2048]{1,0:T(8,128)(2,1)} %fusion.16, bf16[2048,4096]{1,0:T(8,128)(2,1)} %all-gather.17.cloned.1.call-done), kind=kOutput, calls=%fused_computation.84 | convolution fusion | flops 17179869184 | bytes 29360128 | tf_op jit(solution)/shard_map/bsn,nm->bsm/dot_general | solution.py:31
  213.8 61.7 %all-gather.19.cloned.1.call-done = bf16[2048,4096]{1,0:T(8,128)(2,1)} async-done(((bf16[256,4096]{1,0:T(8,128)(2,1)}), bf16[2048,4096]{1,0:T(8,128)(2,1)}) %all-gather.19.cloned.1.call-update) | async-done | bytes 16777232 | tf_op jit(solution)/shard_map/all_gather | solution.py:63
  275.6 22.9 %fusion.52 = bf16[1024,4096]{1,0:T(8,128)(2,1)} fusion(bf16[1024,2048]{1,0:T(8,128)(2,1)} %fusion.16, bf16[2048,4096]{1,0:T(8,128)(2,1)} %all-gather.19.cloned.1.call-done), kind=kOutput, calls=%fused_computation.85 | convolution fusion | flops 17179869184 | bytes 29360128 | tf_op jit(solution)/shard_map/bsn,nm->bsm/dot_general | solution.py:31
  298.4 66.4 %all-gather.21.cloned.1.call-done = bf16[4096,2048]{1,0:T(8,128)(2,1)} async-done(((bf16[4096,256]{1,0:T(8,128)(2,1)}), bf16[4096,2048]{1,0:T(8,128)(2,1)}) %all-gather.21.cloned.1.call-update) | async-done | bytes 16777232 | tf_op jit(solution)/shard_map/all_gather | solution.py:65
  364.9 29.5 %fusion.15 = bf16[1,1024,2048]{2,1,0:T(8,128)(2,1)} fusion(f32[1024,2048]{1,0:T(8,128)} %fusion.32, bf16[4096,2048]{1,0:T(8,128)(2,1)} %all-gather.21.cloned.1.call-done, bf16[1024,4096]{1,0:T(8,128)(2,1)} %fusion.52, bf16[1024,4096]{1,0:T(8,128)(2,1)} %fusion.51), kind=kOutput, calls=%fused_computation.20 | convolution fusion | flops 17217617920 | bytes 46137344 | tf_op jit(solution)/shard_map/bsn,nm->bsm/dot_general | solution.py:31
  394.4 88.0 %all-reduce.2.cloned.1.call-done = bf16[1,1024,2048]{2,1,0:T(8,128)(2,1)} async-done(((bf16[1,1024,2048]{2,1,0:T(8,128)(2,1)}), bf16[1,1024,2048]{2,1,0:T(8,128)(2,1)}) %all-reduce.2.cloned.1.call-update) | async-done | bytes 4194320 | tf_op jit(solution)/shard_map/psum | solution.py:81
  482.4 7.8 %fusion.12 = bf16[1,1024,2048]{2,1,0:T(8,128)(2,1)} fusion(bf16[1,1024,2048]{2,1,0:T(8,128)(2,1)} %param.10, bf16[1,1024,2048]{2,1,0:T(8,128)(2,1)} %all-reduce.2.cloned.1.call-done), kind=kLoop, calls=%fused_computation.17 | loop fusion | flops 8388608 | bytes 12582912 | tf_op jit(solution)/shard_map/convert_element_type | solution.py:82
  (43 shorter events, 5.0 us)
Async XLA Ops:
  6.5 5.2 %copy-start.5 = (s32[1024]{0:T(1024)S(1)}, s32[1024]{0:T(1024)}, u32[]{:S(2)}) copy-start(s32[1024]{0:T(1024)} %param.11) | copy-start | bytes 12292
  6.5 5.2 %copy-start.6 = (f32[256]{0:T(256)S(1)}, f32[256]{0:T(256)}, u32[]{:S(2)}) copy-start(f32[256]{0:T(256)} %param.12) | copy-start | bytes 3076
  6.6 33.1 %all-gather.11.cloned.1.call-start = ((), (), s32[]{:S(2)}) async-start(), calls=%async_computation.1 | async-start | bytes 1179648 | tf_op jit(solution)/shard_map/all_gather | solution.py:60
  7.3 48.6 %all-gather.13.cloned.1.call-start = ((), (), s32[]{:S(2)}) async-start(), calls=%async_computation.2 | async-start | bytes 1179648 | tf_op jit(solution)/shard_map/all_gather | solution.py:61
  8.1 71.8 %all-gather.9.cloned.1.call-start = ((), (), s32[]{:S(2)}) async-start(), calls=%async_computation | async-start | bytes 2359296 | tf_op jit(solution)/shard_map/all_gather | solution.py:59
  8.9 97.0 %all-gather.15.cloned.1.call-start = ((), (), s32[]{:S(2)}) async-start(), calls=%async_computation.3 | async-start | bytes 2359296 | tf_op jit(solution)/shard_map/all_gather | solution.py:64
  9.6 181.4 %all-gather.17.cloned.1.call-start = ((), (), s32[]{:S(2)}) async-start(), calls=%async_computation.4 | async-start | bytes 18874368 | tf_op jit(solution)/shard_map/all_gather | solution.py:62
  10.2 265.4 %all-gather.19.cloned.1.call-start = ((), (), s32[]{:S(2)}) async-start(), calls=%async_computation.5 | async-start | bytes 18874368 | tf_op jit(solution)/shard_map/all_gather | solution.py:63
  10.8 354.0 %all-gather.21.cloned.1.call-start = ((), (), s32[]{:S(2)}) async-start(), calls=%async_computation.6 | async-start | bytes 18874368 | tf_op jit(solution)/shard_map/all_gather | solution.py:65
  11.6 470.7 %all-reduce.2.cloned.1.call-start = ((), (), s32[]{:S(2)}) async-start(), calls=%async_computation.7 | async-start | bytes 8388608 | tf_op jit(solution)/shard_map/psum | solution.py:81
  11.7 22.5 %copy-start = (bf16[1,1024,2048]{2,1,0:T(8,128)(2,1)S(1)}, bf16[1,1024,2048]{2,1,0:T(8,128)(2,1)}, u32[]{:S(2)}) copy-start(bf16[1,1024,2048]{2,1,0:T(8,128)(2,1)} %param.10) | copy-start | bytes 12582916
  87.8 1.2 copy-start.1
  90.4 3.5 copy-start.2
  90.4 3.5 copy-start.3
  90.4 4.2 copy-start.7
  93.9 1.6 copy-start.8
  94.6 1.4 copy-start.4
Sparse Core Ops, SparseCore 0:
  9.0 24.8 all-gather.10
  35.5 20.4 all-gather.12
  57.6 22.3 all-gather.8
  81.4 24.4 all-gather.14
  107.4 83.5 all-gather.16
  192.4 83.1 all-gather.18
  277.2 87.6 all-gather.20
  394.5 87.8 all-reduce.1
where the time goes:
time: 497 us
  waiting for transfers between devices  331 us (67%)
  matrix products  103 us (21%)
  other arithmetic  24.9 us (5%)
  blocking collectives  19.5 us (4%)
  between operations  13.7 us (3%)
  local copies, waits for them, and re-layouts  5.31 us (1%)
    dot_general x7, matrix products, project(): jnp.einsum('bsn,nm->bsm', operand, weight, preferred_element_type=jnp.flo...  97 us
    psum x1, waiting for transfers between devices, local_layer(): branch = lax.psum(branch.astype(jnp.bfloat16), 'tp')  88 us
    all_gather x1, waiting for transfers between devices, local_layer(): wg_full = lax.all_gather(w_gate, 'fsdp', axis=0, tiled=True)  77.8 us
    all_gather x1, waiting for transfers between devices, local_layer(): wd_full = lax.all_gather(w_down, 'fsdp', axis=1, tiled=True)  66.4 us
    all_gather x1, waiting for transfers between devices, local_layer(): wu_full = lax.all_gather(w_up, 'fsdp', axis=0, tiled=True)  61.7 us
    all_gather x1, blocking collectives, local_layer(): gain_full = lax.all_gather(norm_gain, 'fsdp', axis=0, tiled=True)  19.5 us
    all_gather x1, waiting for transfers between devices, local_layer(): wq_full = lax.all_gather(w_query, 'fsdp', axis=0, tiled=True)  19.5 us
  transfers between devices with their start and end apart: 8, of which 7 were waited for; matrix products, arithmetic and copies ran while one was open for 19% of the time, Pallas kernels for 0%

commit v1 on v0

v1 whole, which is shorter than its diff:
```python
import functools

import jax
import jax.numpy as jnp
from jax import lax
from jax.experimental import pallas as pl
from jax.experimental.pallas import tpu as pltpu
from jax.sharding import PartitionSpec as P

NORM_EPS = 1e-6
MESH = pl.DeviceIdType.MESH
A, B = 0, 1
OWN, RIGHT, OPP, LEFT = 0, 1, 2, 3
MT = 512


def dot(a, b):
    return jnp.dot(a, b, preferred_element_type=jnp.float32)


def layer_kernel(dims, x, gain, cos, sin, wq, wk, wv, wg, wu, wo, wd,
                 out, land, dland,
                 xv, h, za, stg, act, cosv, sinv, gl, dstg, part, rs1, s1, rs2, ag,
                 r_ici, r_par, s_ici, s_par, r_d, s_d, s_dp, r_y, s_y, r_g, s_g, lsem, dsem, osem):
    seq, dm, rows, qw, hd, ff, tk, cw, nchunk, half = dims
    n_chips = lax.axis_size("fsdp") // 2
    n_dev = lax.axis_size("fsdp")
    me = lax.axis_index("fsdp")
    t = lax.axis_index("tp")
    chip, core = me // 2, me % 2
    other = 1 - core

    def dev(r, c):
        return 2 * lax.rem(chip + r, n_chips) + c

    right, left, partner = dev(RIGHT, core), dev(LEFT, core), dev(OWN, other)

    def remote(src, dst, ssem, rsem, target):
        return pltpu.make_async_remote_copy(src_ref=src, dst_ref=dst, send_sem=ssem, recv_sem=rsem,
                                            device_id=target, device_id_type=MESH)

    def wait_recv(ref, sem):
        remote(ref, ref, sem, sem, {"fsdp": partner}).wait_recv()

    def wait_send(ref, sem):
        remote(ref, ref, sem, sem, {"fsdp": partner}).wait_send()

    barrier = pltpu.get_barrier_semaphore()
    for d in range(1, 8):
        pl.semaphore_signal(barrier, inc=1, device_id={"fsdp": lax.rem(me + d, n_dev)}, device_id_type=MESH)
    for m in (1, 3):
        pl.semaphore_signal(barrier, inc=1, device_id={"tp": t ^ m}, device_id_type=MESH)
    pl.semaphore_wait(barrier, 9)

    def own_parts(n, first):
        if first:
            return ((wq, slice(None), A, 0, qw), (wk, slice(None), B, 0, hd), (wv, slice(None), B, hd, hd))
        col = pl.multiple_of((n - 1) * cw, cw)
        return ((wg, pl.ds(col, cw), A, 0, cw), (wu, pl.ds(col, cw), B, 0, cw))

    def own_send(n, first=False):
        for target, slot, who in ((right, 0, LEFT), (left, 3, RIGHT)):
            for src, cols, ab, off, width in own_parts(n, first):
                remote(src.at[:, cols], land.at[n, me, ab, :, pl.ds(off, width)],
                       s_ici.at[n, slot + ab], r_ici.at[n, who - 1, ab], {"fsdp": target}).start()
        for src, cols, ab, off, width in own_parts(n, first):
            remote(src.at[:, cols], land.at[n, me, ab, :, pl.ds(off, width)],
                   s_par.at[n, OWN, ab], r_par.at[n, OWN, ab], {"fsdp": partner}).start()

    def pass_on(n, r, ab):
        ref = land.at[n, dev(r, core), ab]
        remote(ref, ref, s_par.at[n, r, ab], r_par.at[n, r, ab], {"fsdp": partner}).start()

    def service(n):
        for r, fwd, target, slot in ((LEFT, A, right, 2), (RIGHT, B, left, 5)):
            for ab in (fwd, 1 - fwd):
                ref = land.at[n, dev(r, core), ab]
                wait_recv(ref, r_ici.at[n, r - 1, ab])
                if ab == fwd:
                    remote(ref, ref, s_ici.at[n, slot], r_ici.at[n, OPP - 1, ab], {"fsdp": target}).start()
                pass_on(n, r, ab)

    def finish(n, first=False):
        for ab in (A, B):
            wait_recv(land.at[n, dev(OPP, core), ab], r_ici.at[n, OPP - 1, ab])
            pass_on(n, OPP, ab)
        for src, cols, ab, off, width in own_parts(n, first):
            pltpu.make_async_copy(src.at[:, cols], stg.at[ab, me, :, pl.ds(off, width)], lsem).start()
        for r in (RIGHT, LEFT, OPP):
            for ab in (A, B):
                f = dev(r, core)
                pltpu.make_async_copy(land.at[n, f, ab], stg.at[ab, f], lsem).start()
        for r in (OWN, RIGHT, LEFT, OPP):
            for ab in (A, B):
                f = dev(r, other)
                wait_recv(land.at[n, f, ab], r_par.at[n, r, ab])
                pltpu.make_async_copy(land.at[n, f, ab], stg.at[ab, f], lsem).start()
        pltpu.make_async_copy(stg, stg, lsem).wait()

    kparts = ((0, ((wd, 0, half),), half), (half, ((wd, half, ff - half), (wo, 0, qw)), tk - half))

    def down_region(f, hh, kk):
        lo, _, size = kparts[kk]
        return dland.at[f, hh, pl.ds(lo, size), :]

    def down_own(hh, kk, target, ssem, rsem):
        pos = kparts[kk][0]
        for src, lo, size in kparts[kk][1]:
            remote(src.at[pl.ds(lo, size), pl.ds(hh * 128, 128)], dland.at[me, hh, pl.ds(pos, size), :],
                   ssem, rsem, {"fsdp": target}).start()
            pos += size

    def down_send(hh_right, kk):
        down_own(hh_right, kk, right, s_d.at[0, hh_right, kk], r_d.at[0, LEFT, hh_right, kk])
        hh_left = 1 - hh_right
        down_own(hh_left, kk, left, s_d.at[1, hh_left, kk], r_d.at[0, RIGHT, hh_left, kk])

    def down_pass(r, hh, kk):
        ref = down_region(dev(r, core), hh, kk)
        wait_recv(ref, r_d.at[0, r, hh, kk])
        remote(ref, ref, s_dp.at[r, hh, kk], r_d.at[1, r, hh, kk], {"fsdp": partner}).start()

    def down_forward(kk):
        for r, hh, target, way in ((LEFT, 0, right, 0), (RIGHT, 1, left, 1)):
            ref = down_region(dev(r, core), hh, kk)
            wait_recv(ref, r_d.at[0, r, hh, kk])
            remote(ref, ref, s_d.at[way, 2, kk], r_d.at[0, OPP, hh, kk], {"fsdp": target}).start()
            remote(ref, ref, s_dp.at[r, hh, kk], r_d.at[1, r, hh, kk], {"fsdp": partner}).start()

    for d in range(1, 8):
        f = lax.rem(me + d, n_dev)
        remote(gain, gl.at[me], s_g.at[d - 1], r_g.at[d - 1], {"fsdp": f}).start()
    own_send(0, True)
    own_send(1)
    loads = (pltpu.make_async_copy(x, xv, osem.at[0]), pltpu.make_async_copy(cos, cosv, osem.at[1]),
             pltpu.make_async_copy(sin, sinv, osem.at[2]), pltpu.make_async_copy(gain, gl.at[me], osem.at[3]))
    for cp in loads:
        cp.start()
    for cp in loads:
        cp.wait()
    for d in range(1, 8):
        wait_recv(gl.at[lax.rem(me + n_dev - d, n_dev)], r_g.at[d - 1])

    def norm_tile(i, _):
        rr = pl.ds(pl.multiple_of(i * 128, 128), 128)
        row = xv[rr, :].astype(jnp.float32)
        centered = row - jnp.mean(row, axis=-1, keepdims=True)
        var = jnp.mean(centered * centered, axis=-1, keepdims=True)
        scaled = centered * lax.rsqrt(var + NORM_EPS)
        for f in range(dm // rows):
            cc = slice(f * rows, (f + 1) * rows)
            h[rr, cc] = (scaled[:, cc] * gl[f]).astype(jnp.bfloat16)
        return _

    lax.fori_loop(0, seq // 128, norm_tile, 0)

    def qkv_tile(i, _):
        rr = pl.ds(pl.multiple_of(i * MT, MT), MT)
        hm = h[rr, :]
        cs, sn = cosv[rr, :], sinv[rr, :]
        q = dot(hm, stg[A].reshape(dm, cw)).astype(jnp.bfloat16).astype(jnp.float32)
        kv = dot(hm, stg[B].reshape(dm, cw)).astype(jnp.bfloat16)
        for vec, base in ((q[:, :hd], 0), (q[:, hd:], hd), (kv[:, :hd].astype(jnp.float32), 2 * hd)):
            a, b = vec[:, :hd // 2], vec[:, hd // 2:]
            act[rr, base:base + hd // 2] = (a * cs - b * sn).astype(jnp.bfloat16)
            act[rr, base + hd // 2:base + hd] = (b * cs + a * sn).astype(jnp.bfloat16)
        act[rr, 3 * hd:] = kv[:, hd:]
        return _

    def attention(head):
        qb = 256

        def block(i, _):
            rr = pl.ds(pl.multiple_of(i * qb, qb), qb)
            s = lax.dot_general(act[rr, head * hd:(head + 1) * hd], act[:, 2 * hd:3 * hd],
                                (((1,), (1,)), ((), ())), preferred_element_type=jnp.float32) * (hd ** -0.5)
            qi = i * qb + lax.broadcasted_iota(jnp.int32, (qb, seq), 0)
            ki = lax.broadcasted_iota(jnp.int32, (qb, seq), 1)
            s = jnp.where(ki <= qi, s, -1e30)
            e = jnp.exp(s - jnp.max(s, axis=-1, keepdims=True))
            p = (e * (1.0 / jnp.sum(e, axis=-1, keepdims=True))).astype(jnp.bfloat16)
            o = dot(p, act[:, 3 * hd:])
            za[rr, ff + head * hd:ff + (head + 1) * hd] = o.astype(jnp.bfloat16)
            return _

        lax.fori_loop(0, seq // qb, block, 0)

    def gate_up(n):
        col = pl.ds(pl.multiple_of((n - 1) * cw, cw), cw)

        def tile(i, _):
            rr = pl.ds(pl.multiple_of(i * MT, MT), MT)
            hm = h[rr, :]
            g = dot(hm, stg[A].reshape(dm, cw)).astype(jnp.bfloat16).astype(jnp.float32)
            u = dot(hm, stg[B].reshape(dm, cw)).astype(jnp.bfloat16).astype(jnp.float32)
            za[rr, col] = (g * jax.nn.sigmoid(g) * u).astype(jnp.bfloat16)
            return _

        lax.fori_loop(0, seq // MT, tile, 0)

    service(0)
    own_send(2)
    service(1)
    own_send(3)
    finish(0, True)
    lax.fori_loop(0, seq // MT, qkv_tile, 0)
    for n in (2, 3):
        service(n)
        own_send(n + 2)
        finish(n - 1)
        gate_up(n - 1)
        attention(n - 2)

    def step(n, _):
        service(n)
        own_send(n + 2)
        finish(n - 1)
        gate_up(n - 1)
        return _

    lax.fori_loop(4, nchunk - 2, step, 0)
    for n, kk in ((nchunk - 2, 0), (nchunk - 1, 1)):
        service(n)
        down_send(0, kk)
        for hh in (0, 1):
            down_own(hh, kk, partner, s_dp.at[OWN, hh, kk], r_d.at[1, OWN, hh, kk])
        finish(n - 1)
        gate_up(n - 1)
    down_forward(0)
    down_send(1, 0)
    finish(nchunk - 1)
    gate_up(nchunk - 1)
    down_forward(1)
    down_send(1, 1)

    def unit_blocks(g, cc):
        if g == 0:
            sel = ((OWN, 0), (OWN, 1))
        elif g == 1:
            sel = ((LEFT, 0), (RIGHT, 1))
        elif g == 2:
            sel = ((OPP, 0), (OPP, 1))
        else:
            sel = ((LEFT, 1), (RIGHT, 0))
        return [(r, dev(r, core if cc == 0 else other), hh) for r, hh in sel]

    def unit_load(g, cc):
        for s, (r, f, hh) in enumerate(unit_blocks(g, cc)):
            dst = dstg.at[cc, :, pl.ds(s * 128, 128)]
            if g == 0 and cc == 0:
                cols = pl.ds(hh * 128, 128)
                pltpu.make_async_copy(wd.at[:, cols], dstg.at[cc, pl.ds(0, ff), pl.ds(s * 128, 128)], dsem.at[cc]).start()
                pltpu.make_async_copy(wo.at[:, cols], dstg.at[cc, pl.ds(ff, qw), pl.ds(s * 128, 128)], dsem.at[cc]).start()
            else:
                if cc == 1:
                    for kk in (0, 1):
                        wait_recv(down_region(f, hh, kk), r_d.at[1, r, hh, kk])
                pltpu.make_async_copy(dland.at[f, hh], dst, dsem.at[cc]).start()

    def unit_wait(cc):
        pltpu.make_async_copy(dstg.at[cc], dstg.at[cc], dsem.at[cc]).wait()

    b0, b1 = t % 2, t // 2

    def y_plan(cc):
        if cc == 0:
            return t ^ 1, t ^ 3, (b0 + b1) % 2, b1
        return t ^ 3, t ^ 1, b1, b0

    hs, qs = seq // 2, seq // 4

    def ds_(start, size):
        return pl.ds(pl.multiple_of(start, size), size)

    for g in range(4):
        if g == 2:
            for kk in (0, 1):
                for hh in (0, 1):
                    down_pass(OPP, hh, kk)
        if g == 3:
            for kk in (0, 1):
                down_pass(LEFT, 1, kk)
                down_pass(RIGHT, 0, kk)
        unit_load(g, 0)
        for cc in (0, 1):
            if cc == 0:
                unit_load(g, 1)
            unit_wait(cc)
            u = 2 * g + cc

            def tile(i, _, cc=cc, u=u):
                rr = pl.ds(pl.multiple_of(i * MT, MT), MT)
                part[u, rr, :] = dot(za[rr, :], dstg[cc]).astype(jnp.bfloat16)
                return _

            lax.fori_loop(0, seq // MT, tile, 0)
            p1, p2, k1, k2 = y_plan(cc)
            remote(part.at[u, ds_((1 - k1) * hs, hs), :], rs1.at[u], s_y.at[u, 0], r_y.at[u, 0], {"tp": p1}).start()
        for cc in (0, 1):
            u = 2 * g + cc
            p1, p2, k1, k2 = y_plan(cc)
            wait_recv(rs1.at[u], r_y.at[u, 0])
            s1[u] = (part[u, ds_(k1 * hs, hs), :].astype(jnp.float32) + rs1[u].astype(jnp.float32)).astype(jnp.bfloat16)
            remote(s1.at[u, ds_((1 - k2) * qs, qs), :], rs2.at[u], s_y.at[u, 1], r_y.at[u, 1], {"tp": p2}).start()
        for cc in (0, 1):
            u = 2 * g + cc
            p1, p2, k1, k2 = y_plan(cc)
            wait_recv(rs2.at[u], r_y.at[u, 1])
            rr = ds_(k1 * hs + k2 * qs, qs)
            tot = s1[u, ds_(k2 * qs, qs), :].astype(jnp.float32) + rs2[u].astype(jnp.float32)
            for s, (r, f, hh) in enumerate(unit_blocks(g, cc)):
                res = xv[rr, ds_(f * 256 + hh * 128, 128)].astype(jnp.float32)
                ag[u, rr, s * 128:(s + 1) * 128] = (res + tot[:, s * 128:(s + 1) * 128]).astype(jnp.bfloat16)
            remote(ag.at[u, rr, :], ag.at[u, rr, :], s_y.at[u, 2], r_y.at[u, 2], {"tp": p2}).start()
        for cc in (0, 1):
            u = 2 * g + cc
            p1, p2, k1, k2 = y_plan(cc)
            wait_recv(ag.at[u, ds_(k1 * hs + (1 - k2) * qs, qs), :], r_y.at[u, 2])
            mine = ag.at[u, ds_(k1 * hs, hs), :]
            remote(mine, mine, s_y.at[u, 3], r_y.at[u, 3], {"tp": p1}).start()
        for cc in (0, 1):
            u = 2 * g + cc
            p1, p2, k1, k2 = y_plan(cc)
            wait_recv(ag.at[u, ds_((1 - k1) * hs, hs), :], r_y.at[u, 3])
            for s, (r, f, hh) in enumerate(unit_blocks(g, cc)):
                pltpu.make_async_copy(ag.at[u, :, pl.ds(s * 128, 128)],
                                      out.at[:, ds_(f * 256 + hh * 128, 128)], osem.at[4]).start()

    pltpu.make_async_copy(ag, ag, osem.at[4]).wait()
    for d in range(1, 8):
        wait_send(gl.at[0], s_g.at[d - 1])

    def drain(n, _):
        for j in range(6):
            wait_send(land.at[0, 0, 0], s_ici.at[n, j])
        for r in range(4):
            for ab in (A, B):
                wait_send(land.at[0, 0, 0], s_par.at[n, r, ab])
        return _

    lax.fori_loop(0, nchunk, drain, 0)
    for kk in (0, 1):
        ref = down_region(0, 0, kk)
        for way in (0, 1):
            for j in range(3):
                wait_send(ref, s_d.at[way, j, kk])
        for r in range(4):
            for hh in (0, 1):
                wait_send(ref, s_dp.at[r, hh, kk])
    for u in range(8):
        for st, ref in enumerate((rs1.at[u], rs2.at[u], rs2.at[u], rs1.at[u])):
            wait_send(ref, s_y.at[u, st])


def solution(mesh):
    row_spec = P(("dp", "fsdp"), None, None)

    def local_layer(hidden, positions, norm_gain, w_query, w_key, w_value, w_gate, w_up, w_out, w_down):
        _, seq, dm = hidden.shape
        rows, qw = w_query.shape
        hd = w_key.shape[1]
        ff = w_gate.shape[1]
        n_dev = dm // rows
        cw = qw
        nchunk = 1 + ff // cw
        tk = ff + qw
        half = ff // 2
        inv_freq = 10000.0 ** (-jnp.arange(0, hd, 2, dtype=jnp.float32) / hd)
        angles = positions.astype(jnp.float32)[:, None] * inv_freq[None, :]
        bf, f32 = jnp.bfloat16, jnp.float32
        dma = pltpu.SemaphoreType.DMA
        dims = (seq, dm, rows, qw, hd, ff, tk, cw, nchunk, half)
        anyspec = pl.BlockSpec(memory_space=pl.ANY)
        out, _, _ = pl.pallas_call(
            functools.partial(layer_kernel, dims),
            out_shape=(jax.ShapeDtypeStruct((seq, dm), bf),
                       jax.ShapeDtypeStruct((nchunk, n_dev, 2, rows, cw), bf),
                       jax.ShapeDtypeStruct((n_dev, 2, tk, 128), bf)),
            in_specs=[anyspec] * 11,
            out_specs=(anyspec,) * 3,
            scratch_shapes=[
                pltpu.VMEM((seq, dm), bf),
                pltpu.VMEM((seq, dm), bf),
                pltpu.VMEM((seq, tk), bf),
                pltpu.VMEM((2, n_dev, rows, cw), bf),
                pltpu.VMEM((seq, 4 * hd), bf),
                pltpu.VMEM((seq, hd // 2), f32),
                pltpu.VMEM((seq, hd // 2), f32),
                pltpu.VMEM((n_dev, 1, rows), f32),
                pltpu.VMEM((2, tk, 256), bf),
                pltpu.VMEM((8, seq, 256), bf),
                pltpu.VMEM((8, seq // 2, 256), bf),
                pltpu.VMEM((8, seq // 2, 256), bf),
                pltpu.VMEM((8, seq // 4, 256), bf),
                pltpu.VMEM((8, seq, 256), bf),
                dma((nchunk, 3, 2)), dma((nchunk, 4, 2)), dma((nchunk, 6)), dma((nchunk, 4, 2)),
                dma((2, 4, 2, 2)), dma((2, 3, 2)), dma((4, 2, 2)),
                dma((8, 4)), dma((8, 4)), dma((7,)), dma((7,)), dma, dma((2,)), dma((5,)),
            ],
            compiler_params=pltpu.CompilerParams(collective_id=0, has_side_effects=True,
                                                 vmem_limit_bytes=67043328),
        )(hidden.reshape(seq, dm), norm_gain.reshape(1, rows), jnp.cos(angles), jnp.sin(angles),
          w_query, w_key, w_value, w_gate, w_up, w_out, w_down)
        return out.reshape(hidden.shape)

    in_specs = (row_spec, P(None), P("fsdp"), P("fsdp", "tp"), P("fsdp", None), P("fsdp", None), P("fsdp", "tp"), P("fsdp", "tp"), P("tp", "fsdp"), P("tp", "fsdp"))
    return jax.shard_map(local_layer, mesh=mesh, in_specs=in_specs, out_specs=row_spec, check_vma=False)
```

time: 497 us -> 322 us (0.65)
  waiting for transfers between devices: 331 us -> 0 us
  Pallas kernels: 0 us -> 312 us
  matrix products: 103 us -> 0 us
  other arithmetic: 24.9 us -> 3.73 us
  blocking collectives: 19.5 us -> 0 us
  between operations: 13.7 us -> 0.01 us
    pallas_call x0 -> x1, Pallas kernels: none -> 312 us  [local_layer(): pl.pallas_call(functools.partial(layer_kernel, dims), out_shape=(jax.Shap...]
    all_gather x7 -> x0, waiting for transfers between devices: 238 us -> none  [the longest x1 77.8 us: local_layer(): wg_full = lax.all_gather(w_gate, 'fsdp', axis=0, tiled=True)]
    dot_general x10 -> x0, matrix products: 99.1 us -> none  [the longest x7 97 us: project(): jnp.einsum('bsn,nm->bsm', operand, weight, preferred_element_type=jnp.flo...]
    psum x1 -> x0, waiting for transfers between devices: 88 us -> none  [local_layer(): branch = lax.psum(branch.astype(jnp.bfloat16), 'tp')]
    all_gather x1 -> x0, blocking collectives: 19.5 us -> none  [local_layer(): gain_full = lax.all_gather(norm_gain, 'fsdp', axis=0, tiled=True)]
    convert_element_type x5 -> x1, other arithmetic: 14.3 us -> 0.69 us  [local_layer(): angles = positions.astype(jnp.float32)[:, None] * inv_freq[None, :]]
  transfers between devices with their start and end apart: 8 -> 0, of which waited for: 7 -> 0; matrix products, arithmetic and copies ran while one was open for 19% -> 0% of each run, Pallas kernels for 0% -> 0%
where the time goes in v1:
time: 322 us; the launch traced here: 321 us
  Pallas kernels  312 us (97%)
  local copies, waits for them, and re-layouts  4.79 us (1%)
  other arithmetic  3.73 us (1%)
    pallas_call x1, Pallas kernels, local_layer(): pl.pallas_call(functools.partial(layer_kernel, dims), out_shape=(jax.Shap...  312 us

profile of v1, /device:TPU:97, one launch (start us, length us, event | category | flops | bytes accessed | tf_op | source)
XLA Modules:
  0.0 321.0 jit_solution(11578051463282621871)
XLA Ops:
  0.0 0.7 convert_element_type.3
  0.7 3.0 multiply_sine_fusion
  3.7 312.5 %shard_map.100 = (bf16[1024,2048]{1,0:T(8,128)(2,1)}, bf16[9,8,2,256,512]{4,3,2,1,0:T(8,128)(2,1)}, bf16[8,2,4608,128]{3,2,1,0:T(8,128)(2,1)}) custom-call(bf16[1024,2048]{1,0:T(8,128)(2,1)} %bitcast.3, f32[1,256]{1,0:T(1,128)} %bitcast.5, f32[1024,128]{1,0:T(8,128)} %get-tuple-element.8.cos, f32[1024,128]{1,0:T(8,128)} %get-tuple-element.7.sin, ...), custom_call_target="tpu_custom_call" | custom-call | tf_op jit(solution)/shard_map/pallas_call | solution.py:374
  316.2 4.8 %copy.12 = bf16[1,1024,2048]{2,1,0:T(8,128)(2,1)} copy(bf16[1,1024,2048]{2,1,0:T(8,128)(2,1)} %bitcast.4) | data formatting | bytes 8388608
  (1 shorter events, 0.0 us)

commit v2 on v1

--- a/solution.py
+++ b/solution.py
@@ -272,7 +272,55 @@
     def ds_(start, size):
         return pl.ds(pl.multiple_of(start, size), size)
 
-    for g in range(4):
+    def compute_unit(g, cc):
+        u = 2 * g + cc
+        unit_wait(cc)
+        p1, _, k1, _ = y_plan(cc)
+        for keep in (False, True):
+            rr = ds_((k1 if keep else 1 - k1) * hs, hs)
+            part[u, rr, :] = dot(za[rr, :], dstg[cc]).astype(jnp.bfloat16)
+            if not keep:
+                remote(part.at[u, rr, :], rs1.at[u], s_y.at[u, 0], r_y.at[u, 0], {"tp": p1}).start()
+
+    def sum_half(g, cc):
+        u = 2 * g + cc
+        _, p2, k1, k2 = y_plan(cc)
+        wait_recv(rs1.at[u], r_y.at[u, 0])
+        s1[u] = (part[u, ds_(k1 * hs, hs), :].astype(jnp.float32) + rs1[u].astype(jnp.float32)).astype(jnp.bfloat16)
+        remote(s1.at[u, ds_((1 - k2) * qs, qs), :], rs2.at[u], s_y.at[u, 1], r_y.at[u, 1], {"tp": p2}).start()
+
+    def sum_quarter(g, cc):
+        u = 2 * g + cc
+        _, p2, k1, k2 = y_plan(cc)
+        wait_recv(rs2.at[u], r_y.at[u, 1])
+        rr = ds_(k1 * hs + k2 * qs, qs)
+        tot = s1[u, ds_(k2 * qs, qs), :].astype(jnp.float32) + rs2[u].astype(jnp.float32)
+        for s, (_, f, hh) in enumerate(unit_blocks(g, cc)):
+            res = xv[rr, ds_(f * 256 + hh * 128, 128)].astype(jnp.float32)
+            ag[u, rr, s * 128:(s + 1) * 128] = (res + tot[:, s * 128:(s + 1) * 128]).astype(jnp.bfloat16)
+        remote(ag.at[u, rr, :], ag.at[u, rr, :], s_y.at[u, 2], r_y.at[u, 2], {"tp": p2}).start()
+
+    def share_half(g, cc):
+        u = 2 * g + cc
+        p1, _, k1, k2 = y_plan(cc)
+        wait_recv(ag.at[u, ds_(k1 * hs + (1 - k2) * qs, qs), :], r_y.at[u, 2])
+        mine = ag.at[u, ds_(k1 * hs, hs), :]
+        remote(mine, mine, s_y.at[u, 3], r_y.at[u, 3], {"tp": p1}).start()
+
+    def store_unit(g, cc):
+        u = 2 * g + cc
+        _, _, k1, _ = y_plan(cc)
+        wait_recv(ag.at[u, ds_((1 - k1) * hs, hs), :], r_y.at[u, 3])
+        for s, (_, f, hh) in enumerate(unit_blocks(g, cc)):
+            pltpu.make_async_copy(ag.at[u, :, pl.ds(s * 128, 128)],
+                                  out.at[:, ds_(f * 256 + hh * 128, 128)], osem.at[4]).start()
+
+    def both(fn, g):
+        if 0 <= g < 4:
+            fn(g, 0)
+            fn(g, 1)
+
+    for g in range(5):
         if g == 2:
             for kk in (0, 1):
                 for hh in (0, 1):
@@ -281,50 +329,12 @@
             for kk in (0, 1):
                 down_pass(LEFT, 1, kk)
                 down_pass(RIGHT, 0, kk)
-        unit_load(g, 0)
-        for cc in (0, 1):
-            if cc == 0:
-                unit_load(g, 1)
-            unit_wait(cc)
-            u = 2 * g + cc
-
-            def tile(i, _, cc=cc, u=u):
-                rr = pl.ds(pl.multiple_of(i * MT, MT), MT)
-                part[u, rr, :] = dot(za[rr, :], dstg[cc]).astype(jnp.bfloat16)
-                return _
-
-            lax.fori_loop(0, seq // MT, tile, 0)
-            p1, p2, k1, k2 = y_plan(cc)
-            remote(part.at[u, ds_((1 - k1) * hs, hs), :], rs1.at[u], s_y.at[u, 0], r_y.at[u, 0], {"tp": p1}).start()
-        for cc in (0, 1):
-            u = 2 * g + cc
-            p1, p2, k1, k2 = y_plan(cc)
-            wait_recv(rs1.at[u], r_y.at[u, 0])
-            s1[u] = (part[u, ds_(k1 * hs, hs), :].astype(jnp.float32) + rs1[u].astype(jnp.float32)).astype(jnp.bfloat16)
-            remote(s1.at[u, ds_((1 - k2) * qs, qs), :], rs2.at[u], s_y.at[u, 1], r_y.at[u, 1], {"tp": p2}).start()
-        for cc in (0, 1):
-            u = 2 * g + cc
-            p1, p2, k1, k2 = y_plan(cc)
-            wait_recv(rs2.at[u], r_y.at[u, 1])
-            rr = ds_(k1 * hs + k2 * qs, qs)
-            tot = s1[u, ds_(k2 * qs, qs), :].astype(jnp.float32) + rs2[u].astype(jnp.float32)
-            for s, (r, f, hh) in enumerate(unit_blocks(g, cc)):
-                res = xv[rr, ds_(f * 256 + hh * 128, 128)].astype(jnp.float32)
-                ag[u, rr, s * 128:(s + 1) * 128] = (res + tot[:, s * 128:(s + 1) * 128]).astype(jnp.bfloat16)
-            remote(ag.at[u, rr, :], ag.at[u, rr, :], s_y.at[u, 2], r_y.at[u, 2], {"tp": p2}).start()
-        for cc in (0, 1):
-            u = 2 * g + cc
-            p1, p2, k1, k2 = y_plan(cc)
-            wait_recv(ag.at[u, ds_(k1 * hs + (1 - k2) * qs, qs), :], r_y.at[u, 2])
-            mine = ag.at[u, ds_(k1 * hs, hs), :]
-            remote(mine, mine, s_y.at[u, 3], r_y.at[u, 3], {"tp": p1}).start()
-        for cc in (0, 1):
-            u = 2 * g + cc
-            p1, p2, k1, k2 = y_plan(cc)
-            wait_recv(ag.at[u, ds_((1 - k1) * hs, hs), :], r_y.at[u, 3])
-            for s, (r, f, hh) in enumerate(unit_blocks(g, cc)):
-                pltpu.make_async_copy(ag.at[u, :, pl.ds(s * 128, 128)],
-                                      out.at[:, ds_(f * 256 + hh * 128, 128)], osem.at[4]).start()
+        both(unit_load, g if g < 4 else -1)
+        both(compute_unit, g if g < 4 else -1)
+        both(share_half, g - 1)
+        both(sum_half, g)
+        both(store_unit, g - 1)
+        both(sum_quarter, g)
 
     pltpu.make_async_copy(ag, ag, osem.at[4]).wait()
     for d in range(1, 8):

time: 322 us -> 311 us (0.966); the launches traced: 321 us -> 306 us
  Pallas kernels: 312 us -> 298 us
    pallas_call x1, Pallas kernels: 312 us -> 298 us  [local_layer(): pl.pallas_call(functools.partial(layer_kernel, dims), out_shape=(jax.Shap...]
where the time goes in v2:
time: 311 us; the launch traced here: 306 us
  Pallas kernels  298 us (96%)
  local copies, waits for them, and re-layouts  4.79 us (2%)
  other arithmetic  3.73 us (1%)
    pallas_call x1, Pallas kernels, local_layer(): pl.pallas_call(functools.partial(layer_kernel, dims), out_shape=(jax.Shap...  298 us

profile of v2, /device:TPU:97, one launch (start us, length us, event | category | flops | bytes accessed | tf_op | source)
XLA Modules:
  0.0 306.2 jit_solution(11075704127656820056)
XLA Ops:
  0.0 0.7 convert_element_type.3
  0.7 3.0 multiply_sine_fusion
  3.7 297.7 %shard_map.100 = (bf16[1024,2048]{1,0:T(8,128)(2,1)}, bf16[9,8,2,256,512]{4,3,2,1,0:T(8,128)(2,1)}, bf16[8,2,4608,128]{3,2,1,0:T(8,128)(2,1)}) custom-call(bf16[1024,2048]{1,0:T(8,128)(2,1)} %bitcast.3, f32[1,256]{1,0:T(1,128)} %bitcast.5, f32[1024,128]{1,0:T(8,128)} %get-tuple-element.8.cos, f32[1024,128]{1,0:T(8,128)} %get-tuple-element.7.sin, ...), custom_call_target="tpu_custom_call" | custom-call | tf_op jit(solution)/shard_map/pallas_call | solution.py:384
  301.4 4.8 %copy.12 = bf16[1,1024,2048]{2,1,0:T(8,128)(2,1)} copy(bf16[1,1024,2048]{2,1,0:T(8,128)(2,1)} %bitcast.4) | data formatting | bytes 8388608
  (1 shorter events, 0.0 us)

commit v3 on v0

v3 whole, which is shorter than its diff:
```python
import functools

import jax
import jax.numpy as jnp
from jax import lax
from jax.experimental import pallas as pl
from jax.experimental.pallas import tpu as pltpu
from jax.sharding import PartitionSpec as P

NORM_EPS = 1e-6
MESH = pl.DeviceIdType.MESH
A, B = 0, 1
OWN, RIGHT, OPP, LEFT = 0, 1, 2, 3
MT = 512
SLOT = {OWN: 0, RIGHT: 1, LEFT: 0, OPP: 1}


def dot(a, b):
    return jnp.dot(a, b, preferred_element_type=jnp.float32)


def layer_kernel(dims, x, gain, cos, sin, wq, wk, wv, wg, wu, wo, wd,
                 out, lq, lg, ld, lo,
                 h, h2, z, z2, stg, act, cosv, sinv, gl, tr, dstg, part, rs1, s1, rs2, xo, xi, xres, ag,
                 rq, pq, sq, tq, rg, pg, sg, tg, rd, pd, sd, td, ro, po, so, to,
                 sh, rt, sf, rh, sa, ra, r_y, s_y, r_x, s_x, r_gain, s_gain, lsem, dsem, osem):
    seq, dm, rows, qw, hd, ff, qc, kc = dims
    nk = qc // kc
    hs, qs = seq // 2, seq // 4
    n_dev = lax.axis_size("fsdp")
    n_chips = n_dev // 2
    me = lax.axis_index("fsdp")
    t = lax.axis_index("tp")
    chip, core = me // 2, me % 2
    other = 1 - core

    def dev(r, c):
        return 2 * lax.rem(chip + r, n_chips) + c

    right, left, partner, opposite = dev(RIGHT, core), dev(LEFT, core), dev(OWN, other), dev(OPP, core)

    def al(start, size):
        return pl.ds(pl.multiple_of(start, size), size)

    def remote(src, dst, ssem, rsem, target):
        return pltpu.make_async_remote_copy(src_ref=src, dst_ref=dst, send_sem=ssem, recv_sem=rsem,
                                            device_id=target, device_id_type=MESH)

    def send(src, dst, ssem, rsem, f):
        remote(src, dst, ssem, rsem, {"fsdp": f}).start()

    def wait_recv(ref, sem):
        remote(ref, ref, sem, sem, {"fsdp": partner}).wait_recv()

    def wait_send(ref, sem):
        remote(ref, ref, sem, sem, {"fsdp": partner}).wait_send()

    b0, b1 = t % 2, t // 2

    def y_plan(cc):
        if cc == 0:
            return t ^ 1, t ^ 3, (b0 + b1) % 2, b1
        return t ^ 3, t ^ 1, b1, b0

    def my_rows(cc):
        _, _, k1, k2 = y_plan(cc)
        return al(k1 * hs + k2 * qs, qs)

    barrier = pltpu.get_barrier_semaphore()
    for d in range(1, 8):
        pl.semaphore_signal(barrier, inc=1, device_id={"fsdp": lax.rem(me + d, n_dev)}, device_id_type=MESH)
    for m in (1, 3):
        pl.semaphore_signal(barrier, inc=1, device_id={"tp": t ^ m}, device_id_type=MESH)
    pl.semaphore_wait(barrier, 9)

    class Ring:
        def __init__(self, region, own, r, p, s, tp_):
            self.region, self.own, self.r, self.p, self.s, self.t = region, own, r, p, s, tp_

        def own_send(self, ab):
            for way, target, who in ((0, right, LEFT), (1, left, RIGHT)):
                for src, dst in self.own(ab):
                    send(src, dst, self.s.at[way, ab], self.r.at[who - 1, ab], target)
            for src, dst in self.own(ab):
                send(src, dst, self.t.at[OWN, ab], self.p.at[OWN, ab], partner)

        def pass_on(self, r, ab):
            ref = self.region(dev(r, core), ab)
            wait_recv(ref, self.r.at[r - 1, ab])
            send(ref, ref, self.t.at[r, ab], self.p.at[r, ab], partner)

        def service(self):
            for r, ab, target, way in ((LEFT, A, right, 0), (RIGHT, B, left, 1)):
                ref = self.region(dev(r, core), ab)
                wait_recv(ref, self.r.at[r - 1, ab])
                send(ref, ref, self.s.at[way, 2], self.r.at[OPP - 1, ab], target)
                send(ref, ref, self.t.at[r, ab], self.p.at[r, ab], partner)
            self.pass_on(LEFT, B)
            self.pass_on(RIGHT, A)

        def last(self):
            self.pass_on(OPP, A)
            self.pass_on(OPP, B)

        def wait_partner(self, r, ab):
            ref = self.region(dev(r, other), ab)
            wait_recv(ref, self.p.at[r, ab])
            return ref

        def drain(self):
            ref = self.region(0, A)
            for j in range(3):
                for way in (0, 1):
                    wait_send(ref, self.s.at[way, j])
            for r in range(4):
                for ab in (A, B):
                    wait_send(ref, self.t.at[r, ab])

    class Pair:
        def __init__(self, region, own, r, p, s, tp_):
            self.region, self.own, self.r, self.p, self.s, self.t = region, own, r, p, s, tp_

        def one(self, q, side, target, ssem, rsem):
            for src, dst in self.own(lax.rem(chip + q, n_chips), side):
                send(src, dst, ssem, rsem, target)

        def own_send(self):
            self.one(1, 0, right, self.s.at[0, 0], self.r.at[LEFT - 1, 0])
            self.one(2, 1, left, self.s.at[1, 0], self.r.at[RIGHT - 1, 1])
            self.one(0, 1, right, self.s.at[0, 1], self.r.at[LEFT - 1, 1])
            self.one(3, 0, left, self.s.at[1, 1], self.r.at[RIGHT - 1, 0])
            self.one(0, 0, partner, self.t.at[OWN, 0], self.p.at[OWN, 0])
            self.one(3, 1, partner, self.t.at[OWN, 1], self.p.at[OWN, 1])

        def pass_on(self, r, side):
            ref = self.region(dev(r, core), side)
            wait_recv(ref, self.r.at[r - 1, side])
            send(ref, ref, self.t.at[r, side], self.p.at[r, side], partner)

        def forward(self):
            for r, side, target, way in ((LEFT, 0, right, 0), (RIGHT, 1, left, 1)):
                f = dev(r, core)
                ref = self.region(f, side)
                wait_recv(ref, self.r.at[r - 1, side])
                send(ref, self.region(f, 1 - side), self.s.at[way, 2], self.r.at[OPP - 1, 1 - side], target)
                send(ref, ref, self.t.at[r, side], self.p.at[r, side], partner)

        def rest(self):
            self.pass_on(LEFT, 1)
            self.pass_on(RIGHT, 0)

        def service(self):
            self.forward()
            self.rest()

        def last(self):
            self.pass_on(OPP, 0)
            self.pass_on(OPP, 1)

        def wait_partner(self, r, side):
            ref = self.region(dev(r, other), side)
            wait_recv(ref, self.p.at[r, side])
            return ref

        def drain(self):
            ref = self.region(0, 0)
            for j in range(3):
                for way in (0, 1):
                    wait_send(ref, self.s.at[way, j])
            for r in range(4):
                for side in (0, 1):
                    wait_send(ref, self.t.at[r, side])

    def qkv_own(ab):
        if ab == A:
            return ((wq, lq.at[me, A]),)
        return ((wk, lq.at[me, B, :, pl.ds(0, hd)]), (wv, lq.at[me, B, :, pl.ds(hd, hd)]))

    qkv = Ring(lambda f, ab: lq.at[f, ab], qkv_own, rq, pq, sq, tq)

    def o_own(ab):
        return ((wo.at[pl.ds(ab * (qw // 2), qw // 2), :], lo.at[me, ab]),)

    w_o = Ring(lambda f, ab: lo.at[f, ab], o_own, ro, po, so, to)

    def gu(k):
        def own(q, side):
            cols = al(q * qc + k * kc, kc)
            return ((wg.at[:, cols], lg.at[k, side, me, A]), (wu.at[:, cols], lg.at[k, side, me, B]))

        return Pair(lambda f, side: lg.at[k, side, f], own, rg.at[k], pg.at[k], sg.at[k], tg.at[k])

    def d_own(q, side):
        return ((wd.at[al(q * qc, qc), :], ld.at[me, side]),)

    w_d = Pair(lambda f, side: ld.at[f, side], d_own, rd, pd, sd, td)

    def local(src, dst, sem):
        pltpu.make_async_copy(src, dst, sem).start()

    def finish_qkv():
        qkv.last()
        for src, cols, ab, off, width in ((wq, None, A, 0, qw), (wk, None, B, 0, hd), (wv, None, B, hd, hd)):
            local(src, stg.at[ab, me, :, pl.ds(off, width)], lsem)
        for ab in (A, B):
            for r in (RIGHT, LEFT, OPP):
                f = dev(r, core)
                local(lq.at[f, ab], stg.at[ab, f], lsem)
            for r in (OWN, RIGHT, LEFT, OPP):
                local(qkv.wait_partner(r, ab), stg.at[ab, dev(r, other)], lsem)
        pltpu.make_async_copy(stg, stg, lsem).wait()

    def finish_gu(k):
        flow = gu(k)
        flow.last()
        for side in (0, 1):
            cols = pl.ds(side * kc, kc)
            q = lax.rem(chip + 3 * side, n_chips)
            for ab, src in ((A, wg), (B, wu)):
                local(src.at[:, al(q * qc + k * kc, kc)], stg.at[ab, me, :, cols], lsem)
            for r in (RIGHT, LEFT, OPP):
                f = dev(r, core)
                for ab in (A, B):
                    local(lg.at[k, side, f, ab], stg.at[ab, f, :, cols], lsem)
            for r in (OWN, RIGHT, LEFT, OPP):
                f = dev(r, other)
                flow.wait_partner(r, side)
                for ab in (A, B):
                    local(lg.at[k, side, f, ab], stg.at[ab, f, :, cols], lsem)
        pltpu.make_async_copy(stg, stg, lsem).wait()

    hc = dm // 2

    def h_cols(cc):
        return pl.ds(cc * hc, hc)

    def rows_out():
        for cc, target in ((0, right), (1, left)):
            send(h.at[my_rows(cc), h_cols(cc)], tr.at[cc], sh.at[cc], rt.at[cc], target)

    def rows_forward():
        for cc, target in ((0, right), (1, left)):
            wait_recv(tr.at[cc], rt.at[cc])
            send(tr.at[cc], h2.at[my_rows(cc), h_cols(cc)], sf.at[cc], rh.at[cc], target)

    def rows_share(step):
        for cc in (0, 1):
            p1, p2, k1, k2 = y_plan(cc)
            if step == 0:
                mine = h2.at[my_rows(cc), h_cols(cc)]
                wait_recv(mine, rh.at[cc])
                remote(mine, mine, sa.at[cc, 0], ra.at[cc, 0], {"tp": p2}).start()
            elif step == 1:
                wait_recv(h2.at[al(k1 * hs + (1 - k2) * qs, qs), h_cols(cc)], ra.at[cc, 0])
                mine = h2.at[al(k1 * hs, hs), h_cols(cc)]
                remote(mine, mine, sa.at[cc, 1], ra.at[cc, 1], {"tp": p1}).start()
            else:
                wait_recv(h2.at[al((1 - k1) * hs, hs), h_cols(cc)], ra.at[cc, 1])

    def norm_tile(i, _):
        rr = al(i * 128, 128)
        blocks = [ag[f, rr, :].astype(jnp.float32) for f in range(dm // rows)]
        mean = sum(jnp.sum(b, axis=-1, keepdims=True) for b in blocks) * (1.0 / dm)
        cent = [b - mean for b in blocks]
        var = sum(jnp.sum(c * c, axis=-1, keepdims=True) for c in cent) * (1.0 / dm)
        scale = lax.rsqrt(var + NORM_EPS)
        for f in range(dm // rows):
            h[rr, f * rows:(f + 1) * rows] = (cent[f] * scale * gl[f]).astype(jnp.bfloat16)
        return _

    def qkv_tile(i, _):
        rr = al(i * MT, MT)
        hm = h[rr, :]
        cs, sn = cosv[rr, :], sinv[rr, :]
        q = dot(hm, stg[A].reshape(dm, qw)).astype(jnp.bfloat16).astype(jnp.float32)
        kv = dot(hm, stg[B].reshape(dm, qw)).astype(jnp.bfloat16)
        for vec, base in ((q[:, :hd], 0), (q[:, hd:], hd), (kv[:, :hd].astype(jnp.float32), 2 * hd)):
            a, b = vec[:, :hd // 2], vec[:, hd // 2:]
            act[rr, base:base + hd // 2] = (a * cs - b * sn).astype(jnp.bfloat16)
            act[rr, base + hd // 2:base + hd] = (b * cs + a * sn).astype(jnp.bfloat16)
        act[rr, 3 * hd:] = kv[:, hd:]
        return _

    def attention(head):
        qb = 256

        def block(i, _):
            rr = al(i * qb, qb)
            s = lax.dot_general(act[rr, head * hd:(head + 1) * hd], act[:, 2 * hd:3 * hd],
                                (((1,), (1,)), ((), ())), preferred_element_type=jnp.float32) * (hd ** -0.5)
            qi = i * qb + lax.broadcasted_iota(jnp.int32, (qb, seq), 0)
            ki = lax.broadcasted_iota(jnp.int32, (qb, seq), 1)
            s = jnp.where(ki <= qi, s, -1e30)
            e = jnp.exp(s - jnp.max(s, axis=-1, keepdims=True))
            p = (e * (1.0 / jnp.sum(e, axis=-1, keepdims=True))).astype(jnp.bfloat16)
            o = dot(p, act[:, 3 * hd:])
            z[rr, 2 * qc + head * hd:2 * qc + (head + 1) * hd] = o.astype(jnp.bfloat16)
            return _

        lax.fori_loop(0, seq // qb, block, 0)

    def gate_up(k, src, dst):
        def tile(i, _):
            rr = al(i * MT, MT)
            hm = src[rr, :]
            g = dot(hm, stg[A].reshape(dm, 2 * kc)).astype(jnp.bfloat16).astype(jnp.float32)
            u = dot(hm, stg[B].reshape(dm, 2 * kc)).astype(jnp.bfloat16).astype(jnp.float32)
            r = (g * jax.nn.sigmoid(g) * u).astype(jnp.bfloat16)
            for side in (0, 1):
                dst[rr, side * qc + k * kc:side * qc + (k + 1) * kc] = r[:, side * kc:(side + 1) * kc]
            return _

        lax.fori_loop(0, seq // MT, tile, 0)

    def unit_f(g, cc):
        return dev(g, core if cc == 0 else other)

    def group_load(g):
        slot = SLOT[g]
        for cc in (0, 1):
            f = unit_f(g, cc)
            cols = pl.ds(cc * rows, rows)
            for side in (0, 1):
                dst = dstg.at[slot, pl.ds(side * qc, qc), cols]
                if g == OWN and cc == 0:
                    local(wd.at[al(lax.rem(chip + 3 * side, n_chips) * qc, qc), :], dst, dsem.at[slot])
                else:
                    if cc == 1:
                        w_d.wait_partner(g, side)
                    local(ld.at[f, side], dst, dsem.at[slot])
            for ab in (A, B):
                dst = dstg.at[slot, pl.ds(2 * qc + ab * (qw // 2), qw // 2), cols]
                if g == OWN and cc == 0:
                    local(wo.at[pl.ds(ab * (qw // 2), qw // 2), :], dst, dsem.at[slot])
                else:
                    if cc == 1:
                        w_o.wait_partner(g, ab)
                    local(lo.at[f, ab], dst, dsem.at[slot])

    def group_compute(g):
        slot = SLOT[g]
        pltpu.make_async_copy(dstg.at[slot], dstg.at[slot], dsem.at[slot]).wait()
        for s, src, depth in ((1, z2, 2 * qc), (0, z, 2 * qc + qw)):
            def tile(i, _, s=s, src=src, depth=depth):
                rr = al(i * MT, MT)
                r = dot(src[rr, :], dstg[slot, :depth, :]).astype(jnp.bfloat16)
                for cc in (0, 1):
                    part[slot, cc, s, rr, :] = r[:, cc * rows:(cc + 1) * rows]
                return _

            lax.fori_loop(0, seq // MT, tile, 0)
        for cc in (0, 1):
            p1, _, k1, _ = y_plan(cc)
            u = 2 * g + cc
            remote(part.at[slot, cc, :, al((1 - k1) * hs, hs), :], rs1.at[u], s_y.at[u, 0], r_y.at[u, 0], {"tp": p1}).start()

    def sum_half(g):
        for cc in (0, 1):
            _, p2, k1, k2 = y_plan(cc)
            u = 2 * g + cc
            wait_recv(rs1.at[u], r_y.at[u, 0])
            s1[u] = (part[SLOT[g], cc, :, al(k1 * hs, hs), :].astype(jnp.float32) + rs1[u].astype(jnp.float32)).astype(jnp.bfloat16)
            remote(s1.at[u, :, al((1 - k2) * qs, qs), :], rs2.at[u], s_y.at[u, 1], r_y.at[u, 1], {"tp": p2}).start()

    def part_free(g):
        for cc in (0, 1):
            wait_send(rs1.at[0], s_y.at[2 * g + cc, 0])

    def sum_quarter(g):
        for cc in (0, 1):
            _, _, _, k2 = y_plan(cc)
            u = 2 * g + cc
            wait_recv(rs2.at[u], r_y.at[u, 1])
            mine = al(k2 * qs, qs)
            xo[u] = (s1[u, 1, mine, :].astype(jnp.float32) + rs2[u, 1].astype(jnp.float32)).astype(jnp.bfloat16)
            f = unit_f(g, cc)
            send(xo.at[u], xi.at[f], s_x.at[u], r_x.at[f], opposite)

    def close(g):
        for cc in (0, 1):
            _, p2, _, k2 = y_plan(cc)
            u = 2 * g + cc
            f = unit_f(g, cc)
            wait_recv(xi.at[f], r_x.at[f])
            mine = al(k2 * qs, qs)
            tot = s1[u, 0, mine, :].astype(jnp.float32) + rs2[u, 0].astype(jnp.float32) + xi[f].astype(jnp.float32)
            ag[u, my_rows(cc), :] = (xres[u].astype(jnp.float32) + tot).astype(jnp.bfloat16)
            ref = ag.at[u, my_rows(cc), :]
            remote(ref, ref, s_y.at[u, 2], r_y.at[u, 2], {"tp": p2}).start()

    def share_half(g):
        for cc in (0, 1):
            p1, _, k1, k2 = y_plan(cc)
            u = 2 * g + cc
            wait_recv(ag.at[u, al(k1 * hs + (1 - k2) * qs, qs), :], r_y.at[u, 2])
            ref = ag.at[u, al(k1 * hs, hs), :]
            remote(ref, ref, s_y.at[u, 3], r_y.at[u, 3], {"tp": p1}).start()

    def store(g):
        for cc in (0, 1):
            _, _, k1, _ = y_plan(cc)
            u = 2 * g + cc
            wait_recv(ag.at[u, al((1 - k1) * hs, hs), :], r_y.at[u, 3])
            local(ag.at[u], out.at[:, al(unit_f(g, cc) * rows, rows)], osem.at[4])

    for d in range(1, 8):
        f = lax.rem(me + d, n_dev)
        send(gain, gl.at[me], s_gain.at[d - 1], r_gain.at[d - 1], f)
    qkv.own_send(A)
    for f in range(dm // rows):
        local(x.at[:, pl.ds(f * rows, rows)], ag.at[f], osem.at[0])
    local(gain, gl.at[me], osem.at[3])
    local(cos, cosv, osem.at[1])
    local(sin, sinv, osem.at[2])
    pltpu.make_async_copy(ag, ag, osem.at[0]).wait()
    pltpu.make_async_copy(gain, gl.at[me], osem.at[3]).wait()
    for d in range(1, 8):
        wait_recv(gl.at[lax.rem(me + n_dev - d, n_dev)], r_gain.at[d - 1])
    lax.fori_loop(0, seq // 128, norm_tile, 0)
    rows_out()
    qkv.own_send(B)
    rows_forward()
    qkv.service()
    gu(0).own_send()
    gu(1).own_send()
    pltpu.make_async_copy(cos, cosv, osem.at[1]).wait()
    pltpu.make_async_copy(sin, sinv, osem.at[2]).wait()
    rows_share(0)
    finish_qkv()
    lax.fori_loop(0, seq // MT, qkv_tile, 0)
    rows_share(1)
    attention(0)
    gu(0).service()
    gu(2).own_send()
    attention(1)
    finish_gu(0)
    gate_up(0, h, z)
    gu(1).service()
    gu(3).own_send()
    rows_share(2)
    gate_up(0, h2, z2)
    gu(2).service()
    w_o.own_send(A)
    w_o.own_send(B)
    finish_gu(1)
    gate_up(1, h, z)
    gate_up(1, h2, z2)
    gu(3).service()
    w_d.own_send()
    finish_gu(2)
    gate_up(2, h, z)
    gate_up(2, h2, z2)
    w_o.service()
    finish_gu(3)
    gate_up(3, h, z)
    gate_up(3, h2, z2)
    w_d.forward()
    group_load(OWN)
    for g in range(4):
        for cc in (0, 1):
            local(x.at[my_rows(cc), al(unit_f(g, cc) * rows, rows)], xres.at[2 * g + cc], osem.at[0])
    group_compute(OWN)
    w_d.rest()
    w_o.last()
    group_load(RIGHT)
    group_compute(RIGHT)
    sum_half(OWN)
    w_d.last()
    group_load(LEFT)
    part_free(OWN)
    sum_half(RIGHT)
    group_compute(LEFT)
    sum_quarter(OWN)
    group_load(OPP)
    part_free(RIGHT)
    group_compute(OPP)
    pltpu.make_async_copy(xres, xres, osem.at[0]).wait()
    sum_quarter(RIGHT)
    sum_half(LEFT)
    sum_half(OPP)
    sum_quarter(LEFT)
    close(RIGHT)
    close(LEFT)
    sum_quarter(OPP)
    share_half(RIGHT)
    share_half(LEFT)
    close(OPP)
    close(OWN)
    store(RIGHT)
    store(LEFT)
    share_half(OPP)
    share_half(OWN)
    store(OPP)
    store(OWN)

    for d in range(1, 8):
        wait_send(gl.at[0], s_gain.at[d - 1])
    for cc in (0, 1):
        wait_send(tr.at[cc], sh.at[cc])
        wait_send(tr.at[cc], sf.at[cc])
        wait_send(h2.at[pl.ds(0, qs), h_cols(0)], sa.at[cc, 0])
        wait_send(h2.at[pl.ds(0, hs), h_cols(0)], sa.at[cc, 1])
    qkv.drain()
    w_o.drain()
    w_d.drain()
    for k in range(nk):
        gu(k).drain()
    for u in range(8):
        if u // 2 in (LEFT, OPP):
            wait_send(rs1.at[u], s_y.at[u, 0])
        wait_send(rs2.at[u], s_y.at[u, 1])
        wait_send(xo.at[u], s_x.at[u])
        wait_send(ag.at[u, pl.ds(0, qs), :], s_y.at[u, 2])
        wait_send(ag.at[u, pl.ds(0, hs), :], s_y.at[u, 3])
    pltpu.make_async_copy(ag, ag, osem.at[4]).wait()


def solution(mesh):
    row_spec = P(("dp", "fsdp"), None, None)

    def local_layer(hidden, positions, norm_gain, w_query, w_key, w_value, w_gate, w_up, w_out, w_down):
        _, seq, dm = hidden.shape
        rows, qw = w_query.shape
        hd = w_key.shape[1]
        ff = w_gate.shape[1]
        n_dev = dm // rows
        qc = ff // (n_dev // 2)
        kc = qw // 2
        nk = qc // kc
        inv_freq = 10000.0 ** (-jnp.arange(0, hd, 2, dtype=jnp.float32) / hd)
        angles = positions.astype(jnp.float32)[:, None] * inv_freq[None, :]
        bf, f32 = jnp.bfloat16, jnp.float32
        dma = pltpu.SemaphoreType.DMA
        dims = (seq, dm, rows, qw, hd, ff, qc, kc)
        anyspec = pl.BlockSpec(memory_space=pl.ANY)
        out = pl.pallas_call(
            functools.partial(layer_kernel, dims),
            out_shape=(jax.ShapeDtypeStruct((seq, dm), bf),
                       jax.ShapeDtypeStruct((n_dev, 2, rows, qw), bf),
                       jax.ShapeDtypeStruct((nk, 2, n_dev, 2, rows, kc), bf),
                       jax.ShapeDtypeStruct((n_dev, 2, qc, rows), bf),
                       jax.ShapeDtypeStruct((n_dev, 2, qw // 2, rows), bf)),
            in_specs=[anyspec] * 11,
            out_specs=(anyspec,) * 5,
            scratch_shapes=[
                pltpu.VMEM((seq, dm), bf),
                pltpu.VMEM((seq, dm), bf),
                pltpu.VMEM((seq, 2 * qc + qw), bf),
                pltpu.VMEM((seq, 2 * qc), bf),
                pltpu.VMEM((2, n_dev, rows, qw), bf),
                pltpu.VMEM((seq, 4 * hd), bf),
                pltpu.VMEM((seq, hd // 2), f32),
                pltpu.VMEM((seq, hd // 2), f32),
                pltpu.VMEM((n_dev, 1, rows), f32),
                pltpu.VMEM((2, seq // 4, dm // 2), bf),
                pltpu.VMEM((2, 2 * qc + qw, 2 * rows), bf),
                pltpu.VMEM((2, 2, 2, seq, rows), bf),
                pltpu.VMEM((8, 2, seq // 2, rows), bf),
                pltpu.VMEM((8, 2, seq // 2, rows), bf),
                pltpu.VMEM((8, 2, seq // 4, rows), bf),
                pltpu.VMEM((8, seq // 4, rows), bf),
                pltpu.VMEM((8, seq // 4, rows), bf),
                pltpu.VMEM((8, seq // 4, rows), bf),
                pltpu.VMEM((8, seq, rows), bf),
                dma((3, 2)), dma((4, 2)), dma((2, 3)), dma((4, 2)),
                dma((nk, 3, 2)), dma((nk, 4, 2)), dma((nk, 2, 3)), dma((nk, 4, 2)),
                dma((3, 2)), dma((4, 2)), dma((2, 3)), dma((4, 2)),
                dma((3, 2)), dma((4, 2)), dma((2, 3)), dma((4, 2)),
                dma((2,)), dma((2,)), dma((2,)), dma((2,)), dma((2, 2)), dma((2, 2)),
                dma((8, 4)), dma((8, 4)), dma((8,)), dma((8,)), dma((7,)), dma((7,)),
                dma, dma((2,)), dma((5,)),
            ],
            compiler_params=pltpu.CompilerParams(collective_id=0, has_side_effects=True,
                                                 vmem_limit_bytes=67043328),
        )(hidden.reshape(seq, dm), norm_gain.reshape(1, rows), jnp.cos(angles), jnp.sin(angles),
          w_query, w_key, w_value, w_gate, w_up, w_out, w_down)[0]
        return out.reshape(hidden.shape)

    in_specs = (row_spec, P(None), P("fsdp"), P("fsdp", "tp"), P("fsdp", None), P("fsdp", None), P("fsdp", "tp"), P("fsdp", "tp"), P("tp", "fsdp"), P("tp", "fsdp"))
    return jax.shard_map(local_layer, mesh=mesh, in_specs=in_specs, out_specs=row_spec, check_vma=False)
```

time: 497 us -> 263 us (0.53)
  waiting for transfers between devices: 331 us -> 0 us
  Pallas kernels: 0 us -> 254 us
  matrix products: 103 us -> 0 us
  other arithmetic: 24.9 us -> 3.72 us
  blocking collectives: 19.5 us -> 0 us
  between operations: 13.7 us -> 0.01 us
    pallas_call x0 -> x1, Pallas kernels: none -> 254 us  [local_layer(): pl.pallas_call(functools.partial(layer_kernel, dims), out_shape=(jax.Shap...]
    all_gather x7 -> x0, waiting for transfers between devices: 238 us -> none  [the longest x1 77.8 us: local_layer(): wg_full = lax.all_gather(w_gate, 'fsdp', axis=0, tiled=True)]
    dot_general x10 -> x0, matrix products: 99.1 us -> none  [the longest x7 97 us: project(): jnp.einsum('bsn,nm->bsm', operand, weight, preferred_element_type=jnp.flo...]
    psum x1 -> x0, waiting for transfers between devices: 88 us -> none  [local_layer(): branch = lax.psum(branch.astype(jnp.bfloat16), 'tp')]
    all_gather x1 -> x0, blocking collectives: 19.5 us -> none  [local_layer(): gain_full = lax.all_gather(norm_gain, 'fsdp', axis=0, tiled=True)]
    convert_element_type x5 -> x1, other arithmetic: 14.3 us -> 0.69 us  [local_layer(): angles = positions.astype(jnp.float32)[:, None] * inv_freq[None, :]]
  transfers between devices with their start and end apart: 8 -> 0, of which waited for: 7 -> 0; matrix products, arithmetic and copies ran while one was open for 19% -> 0% of each run, Pallas kernels for 0% -> 0%
where the time goes in v3:
time: 263 us
  Pallas kernels  254 us (97%)
  local copies, waits for them, and re-layouts  4.79 us (2%)
  other arithmetic  3.72 us (1%)
    pallas_call x1, Pallas kernels, local_layer(): pl.pallas_call(functools.partial(layer_kernel, dims), out_shape=(jax.Shap...  254 us

profile of v3, /device:TPU:97, one launch (start us, length us, event | category | flops | bytes accessed | tf_op | source)
XLA Modules:
  0.0 262.9 jit_solution(14498457770768510206)
XLA Ops:
  0.0 0.7 convert_element_type.3
  0.7 3.0 %multiply_sine_fusion = (f32[1024,128]{1,0:T(8,128)}, f32[1024,128]{1,0:T(8,128)}) fusion(f32[128]{0:T(128)S(1)} %multiply_power_fusion, f32[1024]{0:T(1024)S(1)} %convert_element_type.3), kind=kLoop, calls=%fused_computation | loop fusion | flops 131072 | bytes 1053184 | tf_op jit(solution)/shard_map/sin | solution.py:575
  3.7 254.3 %shard_map.100 = (bf16[1024,2048]{1,0:T(8,128)(2,1)}, bf16[8,2,256,512]{3,2,1,0:T(8,128)(2,1)}, bf16[4,2,8,2,256,256]{5,4,3,2,1,0:T(8,128)(2,1)}, bf16[8,2,1024,...) custom-call(bf16[1024,2048]{1,0:T(8,128)(2,1)} %bitcast.3, f32[1,256]{1,0:T(1,128)} %bitcast.5, ...), custom_call_target="tpu_custom_call" | custom-call | tf_op jit(solution)/shard_map/pallas_call | solution.py:536
  258.1 4.8 %copy.12 = bf16[1,1024,2048]{2,1,0:T(8,128)(2,1)} copy(bf16[1,1024,2048]{2,1,0:T(8,128)(2,1)} %bitcast.4) | data formatting | bytes 8388608
  (1 shorter events, 0.0 us)

commit v4 on v3

--- a/solution.py
+++ b/solution.py
@@ -19,9 +19,9 @@
     return jnp.dot(a, b, preferred_element_type=jnp.float32)
 
 
-def layer_kernel(dims, x, gain, cos, sin, wq, wk, wv, wg, wu, wo, wd,
+def layer_kernel(dims, x, gain, pos, freq, wq, wk, wv, wg, wu, wo, wd,
                  out, lq, lg, ld, lo,
-                 h, h2, z, z2, stg, act, cosv, sinv, gl, tr, dstg, part, rs1, s1, rs2, xo, xi, xres, ag,
+                 h, h2, z, z2, stg, act, posv, freqv, cosv, sinv, gl, tr, dstg, part, rs1, s1, rs2, xo, xi, xres, ag,
                  rq, pq, sq, tq, rg, pg, sg, tg, rd, pd, sd, td, ro, po, so, to,
                  sh, rt, sf, rh, sa, ra, r_y, s_y, r_x, s_x, r_gain, s_gain, lsem, dsem, osem):
     seq, dm, rows, qw, hd, ff, qc, kc = dims
@@ -71,6 +71,11 @@
         pl.semaphore_signal(barrier, inc=1, device_id={"fsdp": lax.rem(me + d, n_dev)}, device_id_type=MESH)
     for m in (1, 3):
         pl.semaphore_signal(barrier, inc=1, device_id={"tp": t ^ m}, device_id_type=MESH)
+    for f in range(dm // rows):
+        pltpu.make_async_copy(x.at[:, pl.ds(f * rows, rows)], ag.at[f], osem.at[0]).start()
+    pltpu.make_async_copy(pos, posv, osem.at[1]).start()
+    pltpu.make_async_copy(freq, freqv, osem.at[2]).start()
+    pltpu.make_async_copy(gain, gl.at[me], osem.at[3]).start()
     pl.semaphore_wait(barrier, 9)
 
     class Ring:
@@ -124,9 +129,11 @@
             for src, dst in self.own(lax.rem(chip + q, n_chips), side):
                 send(src, dst, ssem, rsem, target)
 
-        def own_send(self):
+        def own_first(self):
             self.one(1, 0, right, self.s.at[0, 0], self.r.at[LEFT - 1, 0])
             self.one(2, 1, left, self.s.at[1, 0], self.r.at[RIGHT - 1, 1])
+
+        def own_second(self):
             self.one(0, 1, right, self.s.at[0, 1], self.r.at[LEFT - 1, 1])
             self.one(3, 0, left, self.s.at[1, 1], self.r.at[RIGHT - 1, 0])
             self.one(0, 0, partner, self.t.at[OWN, 0], self.p.at[OWN, 0])
@@ -148,10 +155,6 @@
         def rest(self):
             self.pass_on(LEFT, 1)
             self.pass_on(RIGHT, 0)
-
-        def service(self):
-            self.forward()
-            self.rest()
 
         def last(self):
             self.pass_on(OPP, 0)
@@ -212,21 +215,27 @@
 
     def finish_gu(k):
         flow = gu(k)
-        flow.last()
+
+        def stage(r, mine):
+            f = dev(r, core if mine else other)
+            for side in (0, 1):
+                cols = pl.ds(side * kc, kc)
+                if not mine:
+                    flow.wait_partner(r, side)
+                for ab in (A, B):
+                    local(lg.at[k, side, f, ab], stg.at[ab, f, :, cols], lsem)
+
         for side in (0, 1):
-            cols = pl.ds(side * kc, kc)
             q = lax.rem(chip + 3 * side, n_chips)
             for ab, src in ((A, wg), (B, wu)):
-                local(src.at[:, al(q * qc + k * kc, kc)], stg.at[ab, me, :, cols], lsem)
-            for r in (RIGHT, LEFT, OPP):
-                f = dev(r, core)
-                for ab in (A, B):
-                    local(lg.at[k, side, f, ab], stg.at[ab, f, :, cols], lsem)
-            for r in (OWN, RIGHT, LEFT, OPP):
-                f = dev(r, other)
-                flow.wait_partner(r, side)
-                for ab in (A, B):
-                    local(lg.at[k, side, f, ab], stg.at[ab, f, :, cols], lsem)
+                local(src.at[:, al(q * qc + k * kc, kc)], stg.at[ab, me, :, pl.ds(side * kc, kc)], lsem)
+        stage(RIGHT, True)
+        stage(LEFT, True)
+        stage(OWN, False)
+        flow.last()
+        stage(OPP, True)
+        for r in (RIGHT, LEFT, OPP):
+            stage(r, False)
         pltpu.make_async_copy(stg, stg, lsem).wait()
 
     hc = dm // 2
@@ -266,6 +275,12 @@
         scale = lax.rsqrt(var + NORM_EPS)
         for f in range(dm // rows):
             h[rr, f * rows:(f + 1) * rows] = (cent[f] * scale * gl[f]).astype(jnp.bfloat16)
+        return _
+
+    def rope_tile(i, _):
+        angle = freqv[...] * posv[:, al(i * 128, 128)].astype(jnp.float32)
+        cosv[al(i * 128, 128), :] = jnp.transpose(jnp.cos(angle))
+        sinv[al(i * 128, 128), :] = jnp.transpose(jnp.sin(angle))
         return _
 
     def qkv_tile(i, _):
@@ -328,43 +343,57 @@
                     if cc == 1:
                         w_d.wait_partner(g, side)
                     local(ld.at[f, side], dst, dsem.at[slot])
+
+    def group_load_o(g):
+        slot = SLOT[g]
+        for cc in (0, 1):
+            f = unit_f(g, cc)
             for ab in (A, B):
-                dst = dstg.at[slot, pl.ds(2 * qc + ab * (qw // 2), qw // 2), cols]
+                dst = dstg.at[slot, pl.ds(2 * qc + ab * (qw // 2), qw // 2), pl.ds(cc * rows, rows)]
                 if g == OWN and cc == 0:
-                    local(wo.at[pl.ds(ab * (qw // 2), qw // 2), :], dst, dsem.at[slot])
+                    local(wo.at[pl.ds(ab * (qw // 2), qw // 2), :], dst, dsem.at[2 + slot])
                 else:
                     if cc == 1:
                         w_o.wait_partner(g, ab)
-                    local(lo.at[f, ab], dst, dsem.at[slot])
-
-    def group_compute(g):
+                    local(lo.at[f, ab], dst, dsem.at[2 + slot])
+
+    def group_wait(g, s):
         slot = SLOT[g]
-        pltpu.make_async_copy(dstg.at[slot], dstg.at[slot], dsem.at[slot]).wait()
-        for s, src, depth in ((1, z2, 2 * qc), (0, z, 2 * qc + qw)):
-            def tile(i, _, s=s, src=src, depth=depth):
-                rr = al(i * MT, MT)
-                r = dot(src[rr, :], dstg[slot, :depth, :]).astype(jnp.bfloat16)
-                for cc in (0, 1):
-                    part[slot, cc, s, rr, :] = r[:, cc * rows:(cc + 1) * rows]
-                return _
-
-            lax.fori_loop(0, seq // MT, tile, 0)
+        ref = dstg.at[slot, pl.ds(0, 2 * qc), :] if s else dstg.at[slot, pl.ds(2 * qc, qw), :]
+        pltpu.make_async_copy(ref, ref, dsem.at[2 * (1 - s) + slot]).wait()
+
+    def group_part(g, s):
+        group_wait(g, s)
+        slot = SLOT[g]
+        src, depth = ((z, 2 * qc + qw), (z2, 2 * qc))[s]
+
+        def tile(i, _):
+            rr = al(i * MT, MT)
+            r = dot(src[rr, :], dstg[slot, :depth, :]).astype(jnp.bfloat16)
+            for cc in (0, 1):
+                part[slot, cc, s, rr, :] = r[:, cc * rows:(cc + 1) * rows]
+            return _
+
+        lax.fori_loop(0, seq // MT, tile, 0)
         for cc in (0, 1):
             p1, _, k1, _ = y_plan(cc)
             u = 2 * g + cc
-            remote(part.at[slot, cc, :, al((1 - k1) * hs, hs), :], rs1.at[u], s_y.at[u, 0], r_y.at[u, 0], {"tp": p1}).start()
+            remote(part.at[slot, cc, s, al((1 - k1) * hs, hs), :], rs1.at[u, s],
+                   s_y.at[u, 4 * s], r_y.at[u, 4 * s], {"tp": p1}).start()
 
     def sum_half(g):
         for cc in (0, 1):
             _, p2, k1, k2 = y_plan(cc)
             u = 2 * g + cc
-            wait_recv(rs1.at[u], r_y.at[u, 0])
+            wait_recv(rs1.at[u, 1], r_y.at[u, 4])
+            wait_recv(rs1.at[u, 0], r_y.at[u, 0])
             s1[u] = (part[SLOT[g], cc, :, al(k1 * hs, hs), :].astype(jnp.float32) + rs1[u].astype(jnp.float32)).astype(jnp.bfloat16)
             remote(s1.at[u, :, al((1 - k2) * qs, qs), :], rs2.at[u], s_y.at[u, 1], r_y.at[u, 1], {"tp": p2}).start()
 
     def part_free(g):
         for cc in (0, 1):
-            wait_send(rs1.at[0], s_y.at[2 * g + cc, 0])
+            for st in (0, 4):
+                wait_send(rs1.at[0, 0], s_y.at[2 * g + cc, st])
 
     def sum_quarter(g):
         for cc in (0, 1):
@@ -407,11 +436,6 @@
         f = lax.rem(me + d, n_dev)
         send(gain, gl.at[me], s_gain.at[d - 1], r_gain.at[d - 1], f)
     qkv.own_send(A)
-    for f in range(dm // rows):
-        local(x.at[:, pl.ds(f * rows, rows)], ag.at[f], osem.at[0])
-    local(gain, gl.at[me], osem.at[3])
-    local(cos, cosv, osem.at[1])
-    local(sin, sinv, osem.at[2])
     pltpu.make_async_copy(ag, ag, osem.at[0]).wait()
     pltpu.make_async_copy(gain, gl.at[me], osem.at[3]).wait()
     for d in range(1, 8):
@@ -419,75 +443,93 @@
     lax.fori_loop(0, seq // 128, norm_tile, 0)
     rows_out()
     qkv.own_send(B)
+    pltpu.make_async_copy(pos, posv, osem.at[1]).wait()
+    pltpu.make_async_copy(freq, freqv, osem.at[2]).wait()
+    lax.fori_loop(0, seq // 128, rope_tile, 0)
     rows_forward()
     qkv.service()
-    gu(0).own_send()
-    gu(1).own_send()
-    pltpu.make_async_copy(cos, cosv, osem.at[1]).wait()
-    pltpu.make_async_copy(sin, sinv, osem.at[2]).wait()
+    gu(0).own_first()
+    gu(0).own_second()
+    gu(1).own_first()
     rows_share(0)
     finish_qkv()
     lax.fori_loop(0, seq // MT, qkv_tile, 0)
     rows_share(1)
     attention(0)
-    gu(0).service()
-    gu(2).own_send()
+    gu(0).forward()
+    gu(1).own_second()
+    gu(2).own_first()
+    gu(0).rest()
     attention(1)
     finish_gu(0)
     gate_up(0, h, z)
-    gu(1).service()
-    gu(3).own_send()
+    gu(1).forward()
+    gu(2).own_second()
+    gu(3).own_first()
+    gu(1).rest()
     rows_share(2)
     gate_up(0, h2, z2)
-    gu(2).service()
+    finish_gu(1)
+    gu(2).forward()
+    gu(3).own_second()
+    gate_up(1, h, z)
+    gu(2).rest()
+    gate_up(1, h2, z2)
+    gu(3).forward()
+    w_d.own_first()
+    w_d.own_second()
     w_o.own_send(A)
     w_o.own_send(B)
-    finish_gu(1)
-    gate_up(1, h, z)
-    gate_up(1, h2, z2)
-    gu(3).service()
-    w_d.own_send()
     finish_gu(2)
     gate_up(2, h, z)
+    gu(3).rest()
     gate_up(2, h2, z2)
+    group_load(OWN)
+    group_load_o(OWN)
+    for g in range(4):
+        for cc in (0, 1):
+            local(x.at[my_rows(cc), al(unit_f(g, cc) * rows, rows)], xres.at[2 * g + cc], osem.at[0])
+    finish_gu(3)
+    gate_up(3, h2, z2)
+    group_part(OWN, 1)
+    w_d.forward()
+    gate_up(3, h, z)
+    group_part(OWN, 0)
+    w_d.rest()
+    group_load(RIGHT)
+    group_load(LEFT)
+    group_part(RIGHT, 1)
     w_o.service()
-    finish_gu(3)
-    gate_up(3, h, z)
-    gate_up(3, h2, z2)
-    w_d.forward()
-    group_load(OWN)
-    for g in range(4):
-        for cc in (0, 1):
-            local(x.at[my_rows(cc), al(unit_f(g, cc) * rows, rows)], xres.at[2 * g + cc], osem.at[0])
-    group_compute(OWN)
-    w_d.rest()
+    group_load_o(RIGHT)
+    group_load_o(LEFT)
+    group_part(RIGHT, 0)
+    sum_half(OWN)
+    part_free(OWN)
+    group_part(LEFT, 1)
+    group_part(LEFT, 0)
+    w_d.last()
     w_o.last()
-    group_load(RIGHT)
-    group_compute(RIGHT)
-    sum_half(OWN)
-    w_d.last()
-    group_load(LEFT)
-    part_free(OWN)
+    group_load(OPP)
+    group_load_o(OPP)
     sum_half(RIGHT)
-    group_compute(LEFT)
     sum_quarter(OWN)
-    group_load(OPP)
+    sum_half(LEFT)
     part_free(RIGHT)
-    group_compute(OPP)
+    group_part(OPP, 1)
+    group_part(OPP, 0)
     pltpu.make_async_copy(xres, xres, osem.at[0]).wait()
     sum_quarter(RIGHT)
-    sum_half(LEFT)
+    sum_quarter(LEFT)
+    close(LEFT)
+    close(RIGHT)
     sum_half(OPP)
-    sum_quarter(LEFT)
-    close(RIGHT)
-    close(LEFT)
+    share_half(LEFT)
+    share_half(RIGHT)
     sum_quarter(OPP)
-    share_half(RIGHT)
-    share_half(LEFT)
     close(OPP)
     close(OWN)
+    store(LEFT)
     store(RIGHT)
-    store(LEFT)
     share_half(OPP)
     share_half(OWN)
     store(OPP)
@@ -507,7 +549,8 @@
         gu(k).drain()
     for u in range(8):
         if u // 2 in (LEFT, OPP):
-            wait_send(rs1.at[u], s_y.at[u, 0])
+            wait_send(rs1.at[u, 0], s_y.at[u, 0])
+            wait_send(rs1.at[u, 1], s_y.at[u, 4])
         wait_send(rs2.at[u], s_y.at[u, 1])
         wait_send(xo.at[u], s_x.at[u])
         wait_send(ag.at[u, pl.ds(0, qs), :], s_y.at[u, 2])
@@ -528,7 +571,6 @@
         kc = qw // 2
         nk = qc // kc
         inv_freq = 10000.0 ** (-jnp.arange(0, hd, 2, dtype=jnp.float32) / hd)
-        angles = positions.astype(jnp.float32)[:, None] * inv_freq[None, :]
         bf, f32 = jnp.bfloat16, jnp.float32
         dma = pltpu.SemaphoreType.DMA
         dims = (seq, dm, rows, qw, hd, ff, qc, kc)
@@ -549,6 +591,8 @@
                 pltpu.VMEM((seq, 2 * qc), bf),
                 pltpu.VMEM((2, n_dev, rows, qw), bf),
                 pltpu.VMEM((seq, 4 * hd), bf),
+                pltpu.VMEM((1, seq), jnp.int32),
+                pltpu.VMEM((hd // 2, 1), f32),
                 pltpu.VMEM((seq, hd // 2), f32),
                 pltpu.VMEM((seq, hd // 2), f32),
                 pltpu.VMEM((n_dev, 1, rows), f32),
@@ -567,12 +611,12 @@
                 dma((3, 2)), dma((4, 2)), dma((2, 3)), dma((4, 2)),
                 dma((3, 2)), dma((4, 2)), dma((2, 3)), dma((4, 2)),
                 dma((2,)), dma((2,)), dma((2,)), dma((2,)), dma((2, 2)), dma((2, 2)),
-                dma((8, 4)), dma((8, 4)), dma((8,)), dma((8,)), dma((7,)), dma((7,)),
-                dma, dma((2,)), dma((5,)),
+                dma((8, 5)), dma((8, 5)), dma((8,)), dma((8,)), dma((7,)), dma((7,)),
+                dma, dma((4,)), dma((5,)),
             ],
             compiler_params=pltpu.CompilerParams(collective_id=0, has_side_effects=True,
                                                  vmem_limit_bytes=67043328),
-        )(hidden.reshape(seq, dm), norm_gain.reshape(1, rows), jnp.cos(angles), jnp.sin(angles),
+        )(hidden.reshape(seq, dm), norm_gain.reshape(1, rows), positions.reshape(1, seq), inv_freq.reshape(hd // 2, 1),
           w_query, w_key, w_value, w_gate, w_up, w_out, w_down)[0]
         return out.reshape(hidden.shape)
 

time: 263 us -> 248 us (0.943)
  Pallas kernels: 254 us -> 242 us
  other arithmetic: 3.72 us -> 0.67 us
    pallas_call x1, Pallas kernels: 254 us -> 242 us  [local_layer(): pl.pallas_call(functools.partial(layer_kernel, dims), out_shape=(jax.Shap...]
    sin x1 -> x0, other arithmetic: 3.02 us -> none  [local_layer(): jnp.sin(angles)]
where the time goes in v4:
time: 248 us
  Pallas kernels  242 us (98%)
  local copies, waits for them, and re-layouts  4.79 us (2%)
    pallas_call x1, Pallas kernels, local_layer(): pl.pallas_call(functools.partial(layer_kernel, dims), out_shape=(jax.Shap...  242 us

profile of v4, /device:TPU:97, one launch (start us, length us, event | category | flops | bytes accessed | tf_op | source)
XLA Modules:
  0.0 247.7 jit_solution(4707666946082267373)
XLA Ops:
  0.0 0.7 multiply_power_fusion.freq
  0.7 242.2 %shard_map.100 = (bf16[1024,2048]{1,0:T(8,128)(2,1)}, bf16[8,2,256,512]{3,2,1,0:T(8,128)(2,1)}, bf16[4,2,8,2,256,256]{5,4,3,2,1,0:T(8,128)(2,1)}, bf16[8,2,1024,...) custom-call(bf16[1024,2048]{1,0:T(8,128)(2,1)} %bitcast.4, f32[1,256]{1,0:T(1,128)} %bitcast.7, s32[1,1024]{1,0:T(1,128)} %bitcast.6, ...), custom_call_target="tpu_custom_call" | custom-call | tf_op jit(solution)/shard_map/pallas_call | solution.py:578
  242.9 4.8 %copy.13 = bf16[1,1024,2048]{2,1,0:T(8,128)(2,1)} copy(bf16[1,1024,2048]{2,1,0:T(8,128)(2,1)} %bitcast.5) | data formatting | bytes 8388608

commit v5 on v4

--- a/solution.py
+++ b/solution.py
@@ -22,7 +22,7 @@
 def layer_kernel(dims, x, gain, pos, freq, wq, wk, wv, wg, wu, wo, wd,
                  out, lq, lg, ld, lo,
                  h, h2, z, z2, stg, act, posv, freqv, cosv, sinv, gl, tr, dstg, part, rs1, s1, rs2, xo, xi, xres, ag,
-                 rq, pq, sq, tq, rg, pg, sg, tg, rd, pd, sd, td, ro, po, so, to,
+                 rq, pq, sq, tq, rkv, pkv, skv, tkv, rka, ska, rg, pg, sg, tg, rd, pd, sd, td, ro, po, so, to,
                  sh, rt, sf, rh, sa, ra, r_y, s_y, r_x, s_x, r_gain, s_gain, lsem, dsem, osem):
     seq, dm, rows, qw, hd, ff, qc, kc = dims
     nk = qc // kc
@@ -174,12 +174,50 @@
                 for side in (0, 1):
                     wait_send(ref, self.t.at[r, side])
 
-    def qkv_own(ab):
-        if ab == A:
-            return ((wq, lq.at[me, A]),)
-        return ((wk, lq.at[me, B, :, pl.ds(0, hd)]), (wv, lq.at[me, B, :, pl.ds(hd, hd)]))
-
-    qkv = Ring(lambda f, ab: lq.at[f, ab], qkv_own, rq, pq, sq, tq)
+    half = rows // 2
+
+    def q_region(f, ab):
+        return lq.at[f, A, pl.ds(ab * half, half), :]
+
+    qkv = Ring(q_region, lambda ab: ((wq.at[pl.ds(ab * half, half), :], q_region(me, ab)),), rq, pq, sq, tq)
+
+    kv_cols = ((wk, pl.ds(0, hd)), (wv, pl.ds(hd, hd)))
+    kv_p1, kv_p2 = t ^ (1 + 2 * core), t ^ (3 - 2 * core)
+    kv_k1 = core * b1 + other * lax.rem(b0 + b1, 2)
+    kv_k2 = core * b0 + other * b1
+    kq = rows // 4
+    kv_rows = al(kv_k1 * half + kv_k2 * kq, kq)
+
+    def kv_send():
+        for r, who in ((RIGHT, LEFT), (LEFT, RIGHT), (OPP, OPP)):
+            for src, cols in kv_cols:
+                send(src.at[kv_rows, :], lq.at[me, B, kv_rows, cols], skv.at[r - 1], rkv.at[who - 1], dev(r, core))
+        for src, cols in kv_cols:
+            send(src, lq.at[me, B, :, cols], tkv.at[OWN], pkv.at[OWN], partner)
+
+    def kv_share(step):
+        for r in (RIGHT, OPP, LEFT):
+            f = dev(r, core)
+            if step == 0:
+                ref = lq.at[f, B, kv_rows, :]
+                wait_recv(ref, rkv.at[r - 1])
+                remote(ref, ref, ska.at[0, r - 1], rka.at[0, r - 1], {"tp": kv_p2}).start()
+            elif step == 1:
+                wait_recv(lq.at[f, B, al(kv_k1 * half + (1 - kv_k2) * kq, kq), :], rka.at[0, r - 1])
+                ref = lq.at[f, B, al(kv_k1 * half, half), :]
+                remote(ref, ref, ska.at[1, r - 1], rka.at[1, r - 1], {"tp": kv_p1}).start()
+            else:
+                wait_recv(lq.at[f, B, al((1 - kv_k1) * half, half), :], rka.at[1, r - 1])
+                ref = lq.at[f, B]
+                send(ref, ref, tkv.at[r], pkv.at[r], partner)
+
+    def kv_drain():
+        for r in range(3):
+            wait_send(lq.at[0, B, pl.ds(0, kq), :], skv.at[r])
+            wait_send(lq.at[0, B, pl.ds(0, kq), :], ska.at[0, r])
+            wait_send(lq.at[0, B, pl.ds(0, half), :], ska.at[1, r])
+        for r in range(4):
+            wait_send(lq.at[0, B], tkv.at[r])
 
     def o_own(ab):
         return ((wo.at[pl.ds(ab * (qw // 2), qw // 2), :], lo.at[me, ab]),)
@@ -203,14 +241,19 @@
 
     def finish_qkv():
         qkv.last()
-        for src, cols, ab, off, width in ((wq, None, A, 0, qw), (wk, None, B, 0, hd), (wv, None, B, hd, hd)):
+        for src, ab, off, width in ((wq, A, 0, qw), (wk, B, 0, hd), (wv, B, hd, hd)):
             local(src, stg.at[ab, me, :, pl.ds(off, width)], lsem)
         for ab in (A, B):
             for r in (RIGHT, LEFT, OPP):
                 f = dev(r, core)
                 local(lq.at[f, ab], stg.at[ab, f], lsem)
-            for r in (OWN, RIGHT, LEFT, OPP):
-                local(qkv.wait_partner(r, ab), stg.at[ab, dev(r, other)], lsem)
+        for r in (OWN, RIGHT, LEFT, OPP):
+            f = dev(r, other)
+            for ab in (A, B):
+                qkv.wait_partner(r, ab)
+            wait_recv(lq.at[f, B], pkv.at[r])
+            for ab in (A, B):
+                local(lq.at[f, ab], stg.at[ab, f], lsem)
         pltpu.make_async_copy(stg, stg, lsem).wait()
 
     def finish_gu(k):
@@ -436,42 +479,46 @@
         f = lax.rem(me + d, n_dev)
         send(gain, gl.at[me], s_gain.at[d - 1], r_gain.at[d - 1], f)
     qkv.own_send(A)
+    qkv.own_send(B)
+    kv_send()
     pltpu.make_async_copy(ag, ag, osem.at[0]).wait()
     pltpu.make_async_copy(gain, gl.at[me], osem.at[3]).wait()
     for d in range(1, 8):
         wait_recv(gl.at[lax.rem(me + n_dev - d, n_dev)], r_gain.at[d - 1])
     lax.fori_loop(0, seq // 128, norm_tile, 0)
     rows_out()
-    qkv.own_send(B)
+    qkv.service()
+    kv_share(0)
     pltpu.make_async_copy(pos, posv, osem.at[1]).wait()
     pltpu.make_async_copy(freq, freqv, osem.at[2]).wait()
     lax.fori_loop(0, seq // 128, rope_tile, 0)
+    kv_share(1)
     rows_forward()
-    qkv.service()
     gu(0).own_first()
     gu(0).own_second()
     gu(1).own_first()
-    rows_share(0)
+    kv_share(2)
     finish_qkv()
     lax.fori_loop(0, seq // MT, qkv_tile, 0)
-    rows_share(1)
+    rows_share(0)
     attention(0)
     gu(0).forward()
     gu(1).own_second()
     gu(2).own_first()
+    attention(1)
     gu(0).rest()
-    attention(1)
+    rows_share(1)
     finish_gu(0)
-    gate_up(0, h, z)
     gu(1).forward()
     gu(2).own_second()
     gu(3).own_first()
+    gate_up(0, h, z)
     gu(1).rest()
     rows_share(2)
+    gu(2).forward()
+    gu(3).own_second()
     gate_up(0, h2, z2)
     finish_gu(1)
-    gu(2).forward()
-    gu(3).own_second()
     gate_up(1, h, z)
     gu(2).rest()
     gate_up(1, h2, z2)
@@ -543,6 +590,7 @@
         wait_send(h2.at[pl.ds(0, qs), h_cols(0)], sa.at[cc, 0])
         wait_send(h2.at[pl.ds(0, hs), h_cols(0)], sa.at[cc, 1])
     qkv.drain()
+    kv_drain()
     w_o.drain()
     w_d.drain()
     for k in range(nk):
@@ -607,6 +655,7 @@
                 pltpu.VMEM((8, seq // 4, rows), bf),
                 pltpu.VMEM((8, seq, rows), bf),
                 dma((3, 2)), dma((4, 2)), dma((2, 3)), dma((4, 2)),
+                dma((3,)), dma((4,)), dma((3,)), dma((4,)), dma((2, 3)), dma((2, 3)),
                 dma((nk, 3, 2)), dma((nk, 4, 2)), dma((nk, 2, 3)), dma((nk, 4, 2)),
                 dma((3, 2)), dma((4, 2)), dma((2, 3)), dma((4, 2)),
                 dma((3, 2)), dma((4, 2)), dma((2, 3)), dma((4, 2)),

time: 248 us -> 241 us (0.972)
  Pallas kernels: 242 us -> 235 us
    pallas_call x1, Pallas kernels: 242 us -> 235 us  [local_layer(): pl.pallas_call(functools.partial(layer_kernel, dims), out_shape=(jax.Shap...]
where the time goes in v5:
time: 241 us
  Pallas kernels  235 us (98%)
  local copies, waits for them, and re-layouts  4.79 us (2%)
    pallas_call x1, Pallas kernels, local_layer(): pl.pallas_call(functools.partial(layer_kernel, dims), out_shape=(jax.Shap...  235 us

profile of v5, /device:TPU:97, one launch (start us, length us, event | category | flops | bytes accessed | tf_op | source)
XLA Modules:
  0.0 240.8 jit_solution(7256327061032959570)
XLA Ops:
  0.0 0.7 multiply_power_fusion.freq
  0.7 235.3 %shard_map.100 = (bf16[1024,2048]{1,0:T(8,128)(2,1)}, bf16[8,2,256,512]{3,2,1,0:T(8,128)(2,1)}, bf16[4,2,8,2,256,256]{5,4,3,2,1,0:T(8,128)(2,1)}, bf16[8,2,1024,...) custom-call(bf16[1024,2048]{1,0:T(8,128)(2,1)} %bitcast.4, f32[1,256]{1,0:T(1,128)} %bitcast.7, s32[1,1024]{1,0:T(1,128)} %bitcast.6, ...), custom_call_target="tpu_custom_call" | custom-call | tf_op jit(solution)/shard_map/pallas_call | solution.py:626
  236.0 4.8 %copy.13 = bf16[1,1024,2048]{2,1,0:T(8,128)(2,1)} copy(bf16[1,1024,2048]{2,1,0:T(8,128)(2,1)} %bitcast.5) | data formatting | bytes 8388608

commit v6 on v5

--- a/solution.py
+++ b/solution.py
@@ -571,13 +571,13 @@
     close(RIGHT)
     sum_half(OPP)
     share_half(LEFT)
-    share_half(RIGHT)
     sum_quarter(OPP)
     close(OPP)
+    share_half(RIGHT)
     close(OWN)
+    share_half(OPP)
     store(LEFT)
     store(RIGHT)
-    share_half(OPP)
     share_half(OWN)
     store(OPP)
     store(OWN)
@@ -621,6 +621,7 @@
         inv_freq = 10000.0 ** (-jnp.arange(0, hd, 2, dtype=jnp.float32) / hd)
         bf, f32 = jnp.bfloat16, jnp.float32
         dma = pltpu.SemaphoreType.DMA
+        flow_sems = (dma((3, 2)), dma((4, 2)), dma((2, 3)), dma((4, 2)))
         dims = (seq, dm, rows, qw, hd, ff, qc, kc)
         anyspec = pl.BlockSpec(memory_space=pl.ANY)
         out = pl.pallas_call(
@@ -654,12 +655,12 @@
                 pltpu.VMEM((8, seq // 4, rows), bf),
                 pltpu.VMEM((8, seq // 4, rows), bf),
                 pltpu.VMEM((8, seq, rows), bf),
-                dma((3, 2)), dma((4, 2)), dma((2, 3)), dma((4, 2)),
+                *flow_sems,
                 dma((3,)), dma((4,)), dma((3,)), dma((4,)), dma((2, 3)), dma((2, 3)),
                 dma((nk, 3, 2)), dma((nk, 4, 2)), dma((nk, 2, 3)), dma((nk, 4, 2)),
-                dma((3, 2)), dma((4, 2)), dma((2, 3)), dma((4, 2)),
-                dma((3, 2)), dma((4, 2)), dma((2, 3)), dma((4, 2)),
-                dma((2,)), dma((2,)), dma((2,)), dma((2,)), dma((2, 2)), dma((2, 2)),
+                *flow_sems,
+                *flow_sems,
+                *[dma((2,))] * 4, *[dma((2, 2))] * 2,
                 dma((8, 5)), dma((8, 5)), dma((8,)), dma((8,)), dma((7,)), dma((7,)),
                 dma, dma((4,)), dma((5,)),
             ],

time: 241 us -> 241 us (level)
  no operation moved by 1% of the time
where the time goes in v6:
time: 241 us
  Pallas kernels  236 us (98%)
  local copies, waits for them, and re-layouts  4.79 us (2%)
    pallas_call x1, Pallas kernels, local_layer(): pl.pallas_call(functools.partial(layer_kernel, dims), out_shape=(jax.Shap...  236 us

profile of v6, /device:TPU:97, one launch (start us, length us, event | category | flops | bytes accessed | tf_op | source)
XLA Modules:
  0.0 241.1 jit_solution(8341284723259379843)
XLA Ops:
  0.0 0.7 multiply_power_fusion.freq
  0.7 235.7 %shard_map.100 = (bf16[1024,2048]{1,0:T(8,128)(2,1)}, bf16[8,2,256,512]{3,2,1,0:T(8,128)(2,1)}, bf16[4,2,8,2,256,256]{5,4,3,2,1,0:T(8,128)(2,1)}, bf16[8,2,1024,...) custom-call(bf16[1024,2048]{1,0:T(8,128)(2,1)} %bitcast.4, f32[1,256]{1,0:T(1,128)} %bitcast.7, s32[1,1024]{1,0:T(1,128)} %bitcast.6, ...), custom_call_target="tpu_custom_call" | custom-call | tf_op jit(solution)/shard_map/pallas_call | solution.py:627
  236.4 4.8 %copy.13 = bf16[1,1024,2048]{2,1,0:T(8,128)(2,1)} copy(bf16[1,1024,2048]{2,1,0:T(8,128)(2,1)} %bitcast.5) | data formatting | bytes 8388608

commit v7 on v6

--- a/solution.py
+++ b/solution.py
@@ -493,8 +493,8 @@
     pltpu.make_async_copy(freq, freqv, osem.at[2]).wait()
     lax.fori_loop(0, seq // 128, rope_tile, 0)
     kv_share(1)
+    gu(0).own_first()
     rows_forward()
-    gu(0).own_first()
     gu(0).own_second()
     gu(1).own_first()
     kv_share(2)

time: 241 us -> 245 us (1.017)
  Pallas kernels: 236 us -> 239 us
    pallas_call x1, Pallas kernels: 236 us -> 239 us  [local_layer(): pl.pallas_call(functools.partial(layer_kernel, dims), out_shape=(jax.Shap...]
where the time goes in v7:
time: 245 us
  Pallas kernels  239 us (98%)
  local copies, waits for them, and re-layouts  4.79 us (2%)
    pallas_call x1, Pallas kernels, local_layer(): pl.pallas_call(functools.partial(layer_kernel, dims), out_shape=(jax.Shap...  239 us

profile of v7, /device:TPU:97, one launch (start us, length us, event | category | flops | bytes accessed | tf_op | source)
XLA Modules:
  0.0 244.5 jit_solution(15084507296573550197)
XLA Ops:
  0.0 0.7 multiply_power_fusion.freq
  0.7 239.1 %shard_map.100 = (bf16[1024,2048]{1,0:T(8,128)(2,1)}, bf16[8,2,256,512]{3,2,1,0:T(8,128)(2,1)}, bf16[4,2,8,2,256,256]{5,4,3,2,1,0:T(8,128)(2,1)}, bf16[8,2,1024,...) custom-call(bf16[1024,2048]{1,0:T(8,128)(2,1)} %bitcast.4, f32[1,256]{1,0:T(1,128)} %bitcast.7, s32[1,1024]{1,0:T(1,128)} %bitcast.6, ...), custom_call_target="tpu_custom_call" | custom-call | tf_op jit(solution)/shard_map/pallas_call | solution.py:627
  239.8 4.8 %copy.13 = bf16[1,1024,2048]{2,1,0:T(8,128)(2,1)} copy(bf16[1,1024,2048]{2,1,0:T(8,128)(2,1)} %bitcast.5) | data formatting | bytes 8388608
